TPU v7x, 256 devices: a whole 4x4x8 slice. The times are simulated.
256 devices in a mesh: row: 16 (over z_hi, y, core), col: 16 (over x, z_lo).
Axes of the slice: x: 4, y: 4, z: 8 (z_hi: 2, z_lo: 4; z = z_hi * 4 + z_lo), core: 2. Of those that a mesh axis runs over, the one named last changes fastest.
Arguments:
- constraint_blocks: float32 [64, 32, 256, 256], P('row', 'col'), may hold values from -0.0625 to 0.0625
- factor_blocks: float32 [64, 32, 256, 256], P('row', 'col'), may hold values from -0.0625 to 0.0625
- band_offsets: int32 [16, 2], P('col'), may hold values from 0 to 63, as said below
- block_pattern: int32 [64, 32], P('row', 'col'), may hold values 0 or 1
- cost_linear: float32 [262144], P('col'), may hold values from -6 to 6
- cost_diagonal: float32 [262144], P('col'), may hold values from 0.5 to 4
- lower: float32 [16384], P('row'), may hold values from -1.5 to -0.2
- upper: float32 [16384], P('row'), may hold values from 0.2 to 1.5
- x_start: float32 [262144], P('col'), may hold values from -6 to 6
- z_start: float32 [16384], P('row'), may hold values from -1 to 1
- y_start: float32 [16384], P('row'), may hold values from -0.6 to 0.6
Outputs:
- x_final: float32 [262144], P('col')
- z_final: float32 [16384], P('row')
- y_final: float32 [16384], P('row')
- residuals: float32 [2, 2], replicated
Inputs may be any that keep to these rules, and one draw needn't show every extreme that they name: In each row of band_offsets the 2 offsets are distinct.
All inputs are finite; a program needn't handle non-finite values. No bound on the sum of `block_pattern` on one device may be relied on, other than what follows from the above.
Results may differ from a plain program's by a relative error of at most 0.00016.
Values sent between devices are 32-bit elements; how exact they have to be, the bound alone decides.
No kernel may reach another device: no remote copies, remote signals or barrier semaphores. Data moves between devices by JAX's collectives and lax.ppermute only.
A program may use at most 64 MiB of HBM per device.

v0:
```python
import jax
import jax.numpy as jnp
from jax import lax
from jax.sharding import Mesh
from jax.sharding import PartitionSpec as P

BS = 256
ITERS = 2
CG_STEPS = 2
ROW = ("row_0", "row_1", "row_2")
COL = ("col_0", "col_1")
ROW_COL = ("row_0", "row_1", "row_2", "col_0", "col_1")


sigma_shift = 1e-06
rho_step = 0.1
relaxation = 1.6


def copy_for_each(shard, axis):
    peers = lax.axis_size(axis)
    return lax.all_to_all(
        jnp.broadcast_to(shard[None], (peers, *shard.shape)), axis, 0, 0, tiled=True
    )


def taken_together(shard, axis):
    everything = copy_for_each(shard, axis)
    return jnp.sum(everything, axis=0)


def packed_total(arrays, axis):
    ravelled, at, gathered = (jnp.concatenate([a.reshape(-1) for a in arrays]), 0, [])
    so_far = taken_together(ravelled, axis)
    for a in arrays:
        gathered.append(so_far[at : at + a.size].reshape(a.shape))
        at += a.size
    return tuple(gathered)


def over_pieces(shard, axis):
    pieces = lax.all_gather(shard, axis)
    return pieces.sum(axis=0)


def one_axis_at_a_time(shard, axes):
    for axis in axes:
        shard = lax.pmax(shard, axis)
    return shard


def local(
    constraint_blocks,
    factor_blocks,
    band_offsets,
    block_pattern,
    cost_linear,
    cost_diagonal,
    lower,
    upper,
    x_start,
    z_start,
    y_start,
):
    col_blocks = cost_linear.shape[0] // BS
    row_blocks = lower.shape[0] // BS
    first_row = lax.axis_index(ROW) * row_blocks
    block_rows = first_row + jnp.arange(row_blocks, dtype=jnp.int32)
    columns = (block_rows[:, None] % col_blocks + band_offsets[0][None, :]) % col_blocks
    selector = (
        columns[:, :, None] == jnp.arange(col_blocks, dtype=jnp.int32)[None, None, :]
    ).astype(jnp.float32)
    selector = selector * block_pattern.astype(jnp.float32)[:, :, None]
    shifted = cost_diagonal + sigma_shift

    def forward(blocks, vector):
        vector_blocks = vector.reshape(col_blocks, BS)
        gathered = jnp.einsum(
            "tkc,cb->tkb", selector, vector_blocks, precision=lax.Precision.HIGHEST
        )
        result = jnp.einsum("tkab,tkb->ta", blocks, gathered, precision=lax.Precision.HIGHEST)
        return result.reshape(-1)

    def backward(blocks, vector):
        vector_blocks = vector.reshape(row_blocks, BS)
        contrib = jnp.einsum("tkab,ta->tkb", blocks, vector_blocks, precision=lax.Precision.HIGHEST)
        result = jnp.einsum("tkc,tkb->cb", selector, contrib, precision=lax.Precision.HIGHEST)
        return result.reshape(-1)

    def images(iterate):
        return packed_total(
            (forward(factor_blocks, iterate), forward(constraint_blocks, iterate)), COL
        )

    recorded = []

    def record(iterate, z_value, constraint_image, dual_part):
        primal_local = jnp.max(jnp.abs(constraint_image - z_value))
        dual_local = jnp.max(jnp.abs(cost_diagonal * iterate + cost_linear + dual_part))
        recorded.append((primal_local, dual_local))

    iterate, z_value, y_value = (x_start, z_start, y_start)
    for outer in range(ITERS):
        factor_image, constraint_image = images(iterate)
        gtg_local = backward(factor_blocks, factor_image)
        start_local = (
            backward(constraint_blocks, rho_step * z_value - y_value - rho_step * constraint_image)
            - gtg_local
        )
        if outer == 0:
            start_sum = taken_together(start_local, ROW)
        else:
            start_sum, dual_sum = (
                over_pieces(start_local, ROW),
                over_pieces(gtg_local + backward(constraint_blocks, y_value), ROW),
            )
            record(iterate, z_value, constraint_image, dual_sum)
        remainder = sigma_shift * iterate - cost_linear - shifted * iterate + start_sum
        solved = iterate
        tracked = constraint_image
        direction = jnp.zeros_like(remainder)
        factor_dir = jnp.zeros((row_blocks * BS,), jnp.float32)
        constraint_dir = jnp.zeros((row_blocks * BS,), jnp.float32)
        norm_old = jnp.float32(1.0)
        weighted_dir = jnp.float32(0.0)
        for inner in range(CG_STEPS):
            factor_rem, constraint_rem, norm_now, weighted_rem, weighted_mix = packed_total(
                (
                    forward(factor_blocks, remainder),
                    forward(constraint_blocks, remainder),
                    jnp.sum(remainder * remainder),
                    jnp.sum(remainder * shifted * remainder),
                    jnp.sum(remainder * shifted * direction),
                ),
                COL,
            )
            ratio = norm_now / norm_old
            direction = remainder + ratio * direction
            factor_dir = factor_rem + ratio * factor_dir
            constraint_dir = constraint_rem + ratio * constraint_dir
            weighted_dir = weighted_rem + 2.0 * ratio * weighted_mix + ratio * ratio * weighted_dir
            image_part, squares = packed_total(
                (
                    backward(factor_blocks, factor_dir)
                    + rho_step * backward(constraint_blocks, constraint_dir),
                    jnp.sum(factor_dir * factor_dir)
                    + rho_step * jnp.sum(constraint_dir * constraint_dir),
                ),
                ROW,
            )
            image = image_part + shifted * direction
            step_size = norm_now / (squares + weighted_dir)
            solved = solved + step_size * direction
            remainder = remainder - step_size * image
            tracked = tracked + step_size * constraint_dir
            norm_old = norm_now
        iterate = relaxation * solved + (1.0 - relaxation) * iterate
        blended = relaxation * tracked + (1.0 - relaxation) * z_value
        z_new = jnp.minimum(jnp.maximum(blended + y_value / rho_step, lower), upper)
        y_value = y_value + rho_step * (blended - z_new)
        z_value = z_new
    factor_image, constraint_image = images(iterate)
    dual_sum = taken_together(
        backward(factor_blocks, factor_image) + backward(constraint_blocks, y_value), ROW
    )
    record(iterate, z_value, constraint_image, dual_sum)
    primal_all, dual_all = (
        one_axis_at_a_time(jnp.stack([pair[0] for pair in recorded]), ROW_COL),
        one_axis_at_a_time(jnp.stack([pair[1] for pair in recorded]), ROW_COL),
    )
    residuals = jnp.stack([primal_all, dual_all])
    return (iterate, z_value, y_value, residuals)


def solution(mesh):
    torus = Mesh(mesh.devices.reshape(2, 4, 2, 4, 4), ("row_0", "row_1", "row_2", "col_0", "col_1"))
    in_specs = (
        P(ROW, COL, None, None),
        P(ROW, COL, None, None),
        P(COL, None),
        P(ROW, COL),
        P(COL),
        P(COL),
        P(ROW),
        P(ROW),
        P(COL),
        P(ROW),
        P(ROW),
    )
    out_specs = (P(COL), P(ROW), P(ROW), P())
    return jax.shard_map(local, mesh=torus, in_specs=in_specs, out_specs=out_specs, check_vma=False)
```

profile of v0, /device:TPU:2, one launch (start us, length us, event | category | flops | bytes accessed | tf_op | source)
XLA Modules:
  0.0 545.8 jit_solution(12367420979207901608)
XLA Ops:
  10.1 1.8 fusion.98
  11.9 1.8 fusion.100
  13.8 15.7 %all_to_all.78 = f32[16,1,2048]{2,1,0:T(1,128)S(1)} all-to-all(f32[16,1,2048]{2,1,0:T(1,128)S(1)} %broadcast_in_dim.26), channel_id=1, replica_groups=mesh['row_0'=2,'row_1'=4,'row_2'=2,'col_0'=4,'col_1'=4] {'col_0','col_1'}, dimensions={0} | all-to-all | bytes 262144 | tf_op jit(solution)/shard_map/all_to_all | solution.py:22
  29.7 2.7 fusion.209
  35.1 34.7 %all_to_all.79 = f32[16,1,16384]{2,1,0:T(1,128)S(1)} all-to-all(f32[16,1,16384]{2,1,0:T(1,128)S(1)} %broadcast_in_dim.27), channel_id=1, replica_groups=mesh['row_0'=2,'row_1'=4,'row_2'=2,'col_0'=4,'col_1'=4] {'row_0','row_1'..., dimensions={0} | all-to-all | bytes 2097152 | tf_op jit(solution)/shard_map/all_to_all | solution.py:22
  71.4 1.8 fusion.94
  73.2 1.8 fusion.96
  75.1 2.0 concatenate.34
  77.2 16.7 %all_to_all.80 = f32[16,1,2051]{2,1,0:T(1,128)S(1)} all-to-all(f32[16,1,2051]{2,1,0:T(1,128)S(1)} %broadcast_in_dim.28), channel_id=1, replica_groups=mesh['row_0'=2,'row_1'=4,'row_2'=2,'col_0'=4,'col_1'=4] {'col_0','col_1'}, dimensions={0} | all-to-all | bytes 262528 | tf_op jit(solution)/shard_map/all_to_all | solution.py:22
  101.7 3.8 all-to-all-start.3
  108.7 23.5 %all-to-all-done.3 = f32[16,1,16385]{2,1,0:T(1,128)S(1)} async-done(((f32[16,1,16385]{2,1,0:T(1,128)}), f32[16,1,16385]{2,1,0:T(1,128)S(1)}, u32[]{:S(2)}, u32[]{:S(2)}) %all-to-all-start.3) | async-done | bytes 1048672 | tf_op jit(solution)/shard_map/all_to_all | solution.py:22
  138.4 1.8 fusion.92
  140.3 2.0 concatenate.36
  143.0 9.2 %all-to-all-start.4 = ((f32[16,1,2051]{2,1,0:T(1,128)}), f32[16,1,2051]{2,1,0:T(1,128)S(1)}, u32[]{:S(2)}, u32[]{:S(2)}) async-start(f32[16,1,2051]{2,1,0:T(1,128)} %broadcast_in_dim.30), calls=%async_computation.4 | async-start | bytes 278528 | tf_op jit(solution)/shard_map/all_to_all | solution.py:22
  152.2 7.0 %all-to-all-done.4 = f32[16,1,2051]{2,1,0:T(1,128)S(1)} async-done(((f32[16,1,2051]{2,1,0:T(1,128)}), f32[16,1,2051]{2,1,0:T(1,128)S(1)}, u32[]{:S(2)}, u32[]{:S(2)}) %all-to-all-start.4) | async-done | bytes 131296 | tf_op jit(solution)/shard_map/all_to_all | solution.py:22
  168.2 3.8 all-to-all-start.5
  173.5 25.2 %all-to-all-done.5 = f32[16,1,16385]{2,1,0:T(1,128)S(1)} async-done(((f32[16,1,16385]{2,1,0:T(1,128)}), f32[16,1,16385]{2,1,0:T(1,128)S(1)}, u32[]{:S(2)}, u32[]{:S(2)}) %all-to-all-start.5) | async-done | bytes 1048672 | tf_op jit(solution)/shard_map/all_to_all | solution.py:22
  203.8 1.8 fusion.86
  205.7 1.8 fusion.88
  207.6 16.0 %all_to_all.81 = f32[16,1,2048]{2,1,0:T(1,128)S(1)} all-to-all(f32[16,1,2048]{2,1,0:T(1,128)S(1)} %broadcast_in_dim.32), channel_id=1, replica_groups=mesh['row_0'=2,'row_1'=4,'row_2'=2,'col_0'=4,'col_1'=4] {'col_0','col_1'}, dimensions={0} | all-to-all | bytes 262144 | tf_op jit(solution)/shard_map/all_to_all | solution.py:22
  225.8 2.7 fusion.213
  231.0 50.1 %all-gather.5.cloned.1.call-done = f32[16,1,16384]{2,1,0:T(1,128)} async-done(((f32[1,1,16384]{2,1,0:T(1,128)}), f32[16,1,16384]{2,1,0:T(1,128)}) %all-gather.5.cloned.1.call-update) | async-done | bytes 1048592 | tf_op jit(solution)/shard_map/all_gather | solution.py:42
  281.0 1.9 reduce_sum.332
  283.9 1.8 fusion.82
  285.7 1.8 fusion.84
  287.6 1.9 concatenate.39
  289.6 12.1 %all_to_all.82 = f32[16,1,2051]{2,1,0:T(1,128)S(1)} all-to-all(f32[16,1,2051]{2,1,0:T(1,128)S(1)} %broadcast_in_dim.33), channel_id=1, replica_groups=mesh['row_0'=2,'row_1'=4,'row_2'=2,'col_0'=4,'col_1'=4] {'col_0','col_1'}, dimensions={0} | all-to-all | bytes 262528 | tf_op jit(solution)/shard_map/all_to_all | solution.py:22
  309.8 5.9 %all-to-all-start.8 = ((f32[16,1,16385]{2,1,0:T(1,128)}), f32[16,1,16385]{2,1,0:T(1,128)S(1)}, u32[]{:S(2)}, u32[]{:S(2)}) async-start(f32[16,1,16385]{2,1,0:T(1,128)} %broadcast_in_dim.34), calls=%async_computation.8 | async-start | bytes 2113536 | tf_op jit(solution)/shard_map/all_to_all | solution.py:22
  318.6 23.2 %all-to-all-done.8 = f32[16,1,16385]{2,1,0:T(1,128)S(1)} async-done(((f32[16,1,16385]{2,1,0:T(1,128)}), f32[16,1,16385]{2,1,0:T(1,128)S(1)}, u32[]{:S(2)}, u32[]{:S(2)}) %all-to-all-start.8) | async-done | bytes 1048672 | tf_op jit(solution)/shard_map/all_to_all | solution.py:22
  348.7 1.8 fusion.80
  350.5 1.9 concatenate.41
  353.2 10.0 %all-to-all-start.9 = ((f32[16,1,2051]{2,1,0:T(1,128)}), f32[16,1,2051]{2,1,0:T(1,128)S(1)}, u32[]{:S(2)}, u32[]{:S(2)}) async-start(f32[16,1,2051]{2,1,0:T(1,128)} %broadcast_in_dim.35), calls=%async_computation.9 | async-start | bytes 278528 | tf_op jit(solution)/shard_map/all_to_all | solution.py:22
  363.3 7.0 %all-to-all-done.9 = f32[16,1,2051]{2,1,0:T(1,128)S(1)} async-done(((f32[16,1,2051]{2,1,0:T(1,128)}), f32[16,1,2051]{2,1,0:T(1,128)S(1)}, u32[]{:S(2)}, u32[]{:S(2)}) %all-to-all-start.9) | async-done | bytes 131296 | tf_op jit(solution)/shard_map/all_to_all | solution.py:22
  374.7 2.7 fusion.106
  380.3 3.9 all-to-all-start.10
  385.5 25.4 %all-to-all-done.10 = f32[16,1,16385]{2,1,0:T(1,128)S(1)} async-done(((f32[16,1,16385]{2,1,0:T(1,128)}), f32[16,1,16385]{2,1,0:T(1,128)S(1)}, u32[]{:S(2)}, u32[]{:S(2)}) %all-to-all-start.10) | async-done | bytes 1048672 | tf_op jit(solution)/shard_map/all_to_all | solution.py:22
  420.5 9.2 %all-to-all-start.11 = ((f32[16,1,2048]{2,1,0:T(1,128)}), f32[16,1,2048]{2,1,0:T(1,128)S(1)}, u32[]{:S(2)}, u32[]{:S(2)}) async-start(f32[16,1,2048]{2,1,0:T(1,128)} %broadcast_in_dim.37), calls=%async_computation.11 | async-start | bytes 262144 | tf_op jit(solution)/shard_map/all_to_all | solution.py:22
  431.9 4.8 all-to-all-done.11
  438.1 2.7 fusion.217
  442.7 1.8 broadcast_in_dim.38
  444.5 3.7 all-to-all-start.12
  448.2 42.4 %all-gather.7.cloned.1.call-done = f32[16,1,16384]{2,1,0:T(1,128)} async-done(((f32[1,1,16384]{2,1,0:T(1,128)}), f32[16,1,16384]{2,1,0:T(1,128)}) %all-gather.7.cloned.1.call-update) | async-done | bytes 1048592 | tf_op jit(solution)/shard_map/all_gather | solution.py:42
  490.6 1.9 reduce_sum.348
  496.7 8.8 %all-reduce.4 = (f32[2]{0:T(128)S(1)}, f32[2]{0:T(128)S(1)}) all-reduce(f32[2]{0:T(128)S(1)} %pad_maximum_fusion.9, f32[2]{0:T(128)S(1)} %pad_maximum_fusion.8), channel_id=1, replica_groups=mesh['row_0'=2,'row_1'=4,'row_2'=2,'col_0'=4,'col_1'=4] {'row_0'}, use_global_device_ids=true, to_apply=%region_44.45 | all-reduce | flops 4 | bytes 32 | tf_op jit(solution)/shard_map/pmax | solution.py:48
  505.5 10.1 %all-reduce.2 = (f32[2]{0:T(128)S(1)}, f32[2]{0:T(128)S(1)}) all-reduce(f32[2]{0:T(128)S(1)} %get-tuple-element.30, f32[2]{0:T(128)S(1)} %get-tuple-element.31), channel_id=1, replica_groups=mesh['row_0'=2,'row_1'=4,'row_2'=2,'col_0'=4,'col_1'=4] {'row_1'}, use_global_device_ids=true, to_apply=%region_45.46 | all-reduce | flops 4 | bytes 32 | tf_op jit(solution)/shard_map/pmax | solution.py:48
  515.6 2.5 all-reduce.3
  518.1 9.2 %all-reduce.1 = (f32[2]{0:T(128)S(1)}, f32[2]{0:T(128)S(1)}) all-reduce(f32[2]{0:T(128)S(1)} %get-tuple-element.28, f32[2]{0:T(128)S(1)} %get-tuple-element.29), channel_id=1, replica_groups=mesh['row_0'=2,'row_1'=4,'row_2'=2,'col_0'=4,'col_1'=4] {'col_0'}, use_global_device_ids=true, to_apply=%region_47.48 | all-reduce | flops 4 | bytes 32 | tf_op jit(solution)/shard_map/pmax | solution.py:48
  527.3 10.6 %all-reduce = (f32[1,2]{1,0:T(1,128)S(1)}, f32[1,2]{1,0:T(1,128)S(1)}) all-reduce(f32[1,2]{1,0:T(1,128)S(1)} %bitcast.364, f32[1,2]{1,0:T(1,128)S(1)} %bitcast.365), channel_id=1, replica_groups=mesh['row_0'=2,'row_1'=4,'row_2'=2,'col_0'=4,'col_1'=4] {'col_1'}, use_global_device_ids=true, to_apply=%region_48.49 | all-reduce | flops 4 | bytes 32 | tf_op jit(solution)/shard_map/pmax | solution.py:48
  (260 shorter events, 70.2 us)
Async XLA Ops:
  8.0 90.5 %copy-start.19 = (f32[4,2]{0,1:T(2,128)}, f32[4,2]{0,1:T(2,128)S(1)}, u32[]{:S(2)}) copy-start(f32[4,2]{0,1:T(2,128)S(1)} %convert_element_type.4) | copy-start | bytes 100
  8.9 3.0 copy-start.1
  9.8 88.7 %copy-start.23 = (s32[4,2]{0,1:T(2,128)}, s32[4,2]{0,1:T(2,128)S(1)}, u32[]{:S(2)}) copy-start(s32[4,2]{0,1:T(2,128)S(1)} %and_select_fusion) | copy-start | bytes 100
  10.0 19.6 %copy-start.41 = (f32[1024]{0:T(1024)S(1)}, f32[1024]{0:T(1024)}, u32[]{:S(2)}) copy-start(f32[1024]{0:T(1024)} %param.21) | copy-start | bytes 12292
  10.0 19.6 %copy-start.49 = (f32[1024]{0:T(1024)S(1)}, f32[1024]{0:T(1024)}, u32[]{:S(2)}) copy-start(f32[1024]{0:T(1024)} %param.20) | copy-start | bytes 12292
  29.7 3.8 copy-start.37
  34.2 36.2 %copy-start.11 = (f32[16384]{0:T(1024)S(1)}, f32[16384]{0:T(1024)}, u32[]{:S(2)}) copy-start(f32[16384]{0:T(1024)} %param.16) | copy-start | bytes 196612
  34.3 36.2 %copy-start.12 = (f32[16384]{0:T(1024)S(1)}, f32[16384]{0:T(1024)}, u32[]{:S(2)}) copy-start(f32[16384]{0:T(1024)} %param.15) | copy-start | bytes 196612
  34.3 36.2 %copy-start.13 = (f32[16384]{0:T(1024)S(1)}, f32[16384]{0:T(1024)}, u32[]{:S(2)}) copy-start(f32[16384]{0:T(1024)} %param.19) | copy-start | bytes 196612
  101.7 34.7 %copy-start.20 = (f32[4,2]{0,1:T(2,128)S(1)}, f32[4,2]{0,1:T(2,128)}, u32[]{:S(2)}) copy-start(f32[4,2]{0,1:T(2,128)} %copy-done.19) | copy-start | bytes 100
  101.7 34.7 %copy-start.24 = (s32[4,2]{0,1:T(2,128)S(1)}, s32[4,2]{0,1:T(2,128)}, u32[]{:S(2)}) copy-start(s32[4,2]{0,1:T(2,128)} %copy-done.23) | copy-start | bytes 100
  101.7 30.6 %all-to-all-start.3 = ((f32[16,1,16385]{2,1,0:T(1,128)}), f32[16,1,16385]{2,1,0:T(1,128)S(1)}, u32[]{:S(2)}, u32[]{:S(2)}) async-start(f32[16,1,16385]{2,1,0:T(1,128)} %broadcast_in_dim.29), calls=%async_computation.3 | async-start | bytes 2113536 | tf_op jit(solution)/shard_map/all_to_all | solution.py:22
  136.6 15.6 %copy-start.31 = (f32[1024]{0:T(1024)S(1)}, f32[1024]{0:T(1024)}, u32[]{:S(2)}) copy-start(f32[1024]{0:T(1024)} %copy-done.30) | copy-start | bytes 12292
  143.0 16.3 %all-to-all-start.4 = ((f32[16,1,2051]{2,1,0:T(1,128)}), f32[16,1,2051]{2,1,0:T(1,128)S(1)}, u32[]{:S(2)}, u32[]{:S(2)}) async-start(f32[16,1,2051]{2,1,0:T(1,128)} %broadcast_in_dim.30), calls=%async_computation.4 | async-start | bytes 278528 | tf_op jit(solution)/shard_map/all_to_all | solution.py:22
  159.4 5.9 %copy-start.36 = (f32[2051]{0:T(1024)}, f32[2051]{0:T(1024)S(1)}, u32[]{:S(2)}) copy-start(f32[2051]{0:T(1024)S(1)} %reduce_sum.327) | copy-start | bytes 24616
  168.2 34.5 %copy-start.21 = (f32[4,2]{0,1:T(2,128)S(1)}, f32[4,2]{0,1:T(2,128)}, u32[]{:S(2)}) copy-start(f32[4,2]{0,1:T(2,128)} %copy-done.19) | copy-start | bytes 100
  168.2 30.6 %all-to-all-start.5 = ((f32[16,1,16385]{2,1,0:T(1,128)}), f32[16,1,16385]{2,1,0:T(1,128)S(1)}, u32[]{:S(2)}, u32[]{:S(2)}) async-start(f32[16,1,16385]{2,1,0:T(1,128)} %broadcast_in_dim.31), calls=%async_computation.5 | async-start | bytes 2113536 | tf_op jit(solution)/shard_map/all_to_all | solution.py:22
  172.0 109.0 %all-gather.5.cloned.1.call-start = ((), (), s32[]{:S(2)}) async-start(), calls=%async_computation.13 | async-start | bytes 1114112 | tf_op jit(solution)/shard_map/all_gather | solution.py:42
  202.7 3.0 copy-start.6
  203.8 20.0 %copy-start.38 = (f32[2048]{0:T(1024)S(1)}, f32[2048]{0:T(1024)}, u32[]{:S(2)}) copy-start(f32[2048]{0:T(1024)} %copy-done.37) | copy-start | bytes 24580
  203.8 20.0 %copy-start.42 = (f32[1024]{0:T(1024)S(1)}, f32[1024]{0:T(1024)}, u32[]{:S(2)}) copy-start(f32[1024]{0:T(1024)} %param.21) | copy-start | bytes 12292
  203.8 20.0 %copy-start.45 = (f32[1024]{0:T(1024)S(1)}, f32[1024]{0:T(1024)}, u32[]{:S(2)}) copy-start(f32[1024]{0:T(1024)} %param.18) | copy-start | bytes 12292
  203.8 20.0 %copy-start.47 = (f32[1024]{0:T(1024)S(1)}, f32[1024]{0:T(1024)}, u32[]{:S(2)}) copy-start(f32[1024]{0:T(1024)} %param.17) | copy-start | bytes 12292
  203.8 20.0 %copy-start.50 = (f32[1024]{0:T(1024)S(1)}, f32[1024]{0:T(1024)}, u32[]{:S(2)}) copy-start(f32[1024]{0:T(1024)} %param.20) | copy-start | bytes 12292
  223.8 4.7 copy-start.28
  225.2 3.3 copy-start.39
  225.8 3.8 copy-start.25
  229.9 51.1 %copy-start.17 = (f32[64,256]{1,0:T(8,128)}, f32[64,256]{1,0:T(8,128)S(1)}, u32[]{:S(2)}) copy-start(f32[64,256]{1,0:T(8,128)S(1)} %convolution_bitcast_fusion.7) | copy-start | bytes 196612
  303.6 3.3 copy-start.32
  309.8 32.0 %all-to-all-start.8 = ((f32[16,1,16385]{2,1,0:T(1,128)}), f32[16,1,16385]{2,1,0:T(1,128)S(1)}, u32[]{:S(2)}, u32[]{:S(2)}) async-start(f32[16,1,16385]{2,1,0:T(1,128)} %broadcast_in_dim.34), calls=%async_computation.8 | async-start | bytes 2113536 | tf_op jit(solution)/shard_map/all_to_all | solution.py:22
  346.8 16.4 %copy-start.33 = (f32[1024]{0:T(1024)S(1)}, f32[1024]{0:T(1024)}, u32[]{:S(2)}) copy-start(f32[1024]{0:T(1024)} %copy-done.32) | copy-start | bytes 12292
  353.2 17.1 %all-to-all-start.9 = ((f32[16,1,2051]{2,1,0:T(1,128)}), f32[16,1,2051]{2,1,0:T(1,128)S(1)}, u32[]{:S(2)}, u32[]{:S(2)}) async-start(f32[16,1,2051]{2,1,0:T(1,128)} %broadcast_in_dim.35), calls=%async_computation.9 | async-start | bytes 278528 | tf_op jit(solution)/shard_map/all_to_all | solution.py:22
  370.4 7.0 %copy-start.35 = (f32[2051]{0:T(1024)}, f32[2051]{0:T(1024)S(1)}, u32[]{:S(2)}) copy-start(f32[2051]{0:T(1024)S(1)} %reduce_sum.343) | copy-start | bytes 24616
  373.5 3.8 copy-start.26
  380.3 30.7 %all-to-all-start.10 = ((f32[16,1,16385]{2,1,0:T(1,128)}), f32[16,1,16385]{2,1,0:T(1,128)S(1)}, u32[]{:S(2)}, u32[]{:S(2)}) async-start(f32[16,1,16385]{2,1,0:T(1,128)} %broadcast_in_dim.36), calls=%async_computation.10 | async-start | bytes 2113536 | tf_op jit(solution)/shard_map/all_to_all | solution.py:22
  414.9 79.7 %copy-start.14 = (f32[16384]{0:T(1024)}, f32[16384]{0:T(1024)S(1)}, u32[]{:S(2)}) copy-start(f32[16384]{0:T(1024)S(1)} %multiply_add_fusion) | copy-start | bytes 196612
  416.0 13.7 %copy-start.34 = (f32[1024]{0:T(1024)S(1)}, f32[1024]{0:T(1024)}, u32[]{:S(2)}) copy-start(f32[1024]{0:T(1024)} %get-tuple-element.45) | copy-start | bytes 12292
  417.8 13.0 %copy-start.18 = (f32[64,256]{1,0:T(8,128)S(1)}, f32[64,256]{1,0:T(8,128)}, u32[]{:S(2)}) copy-start(f32[64,256]{1,0:T(8,128)} %copy-done.17) | copy-start | bytes 196612
  417.8 13.0 %copy-start.27 = (s32[4,2]{0,1:T(2,128)S(1)}, s32[4,2]{0,1:T(2,128)}, u32[]{:S(2)}) copy-start(s32[4,2]{0,1:T(2,128)} %copy-done.23) | copy-start | bytes 100
  417.9 19.0 %copy-start.29 = (f32[2048]{0:T(1024)S(1)}, f32[2048]{0:T(1024)}, u32[]{:S(2)}) copy-start(f32[2048]{0:T(1024)} %copy-done.28) | copy-start | bytes 24580
  417.9 19.0 %copy-start.40 = (f32[1024]{0:T(1024)S(1)}, f32[1024]{0:T(1024)}, u32[]{:S(2)}) copy-start(f32[1024]{0:T(1024)} %copy-done.39) | copy-start | bytes 12292
  417.9 19.0 %copy-start.46 = (f32[1024]{0:T(1024)S(1)}, f32[1024]{0:T(1024)}, u32[]{:S(2)}) copy-start(f32[1024]{0:T(1024)} %param.18) | copy-start | bytes 12292
  417.9 19.0 %copy-start.48 = (f32[1024]{0:T(1024)S(1)}, f32[1024]{0:T(1024)}, u32[]{:S(2)}) copy-start(f32[1024]{0:T(1024)} %param.17) | copy-start | bytes 12292
  420.5 16.2 %all-to-all-start.11 = ((f32[16,1,2048]{2,1,0:T(1,128)}), f32[16,1,2048]{2,1,0:T(1,128)S(1)}, u32[]{:S(2)}, u32[]{:S(2)}) async-start(f32[16,1,2048]{2,1,0:T(1,128)} %broadcast_in_dim.37), calls=%async_computation.11 | async-start | bytes 262144 | tf_op jit(solution)/shard_map/all_to_all | solution.py:22
  429.7 60.9 %all-gather.7.cloned.1.call-start = ((), (), s32[]{:S(2)}) async-start(), calls=%async_computation.14 | async-start | bytes 1114112 | tf_op jit(solution)/shard_map/all_gather | solution.py:42
  438.1 3.8 copy-start.44
  440.8 3.7 copy-start.43
  444.5 49.4 %all-to-all-start.12 = ((f32[16,1,16384]{2,1,0:T(1,128)}), f32[16,1,16384]{2,1,0:T(1,128)S(1)}, u32[]{:S(2)}, u32[]{:S(2)}) async-start(f32[16,1,16384]{2,1,0:T(1,128)} %broadcast_in_dim.38), calls=%async_computation.12 | async-start | bytes 2097152 | tf_op jit(solution)/shard_map/all_to_all | solution.py:22
  (13 other events, 27.1 us)
Sparse Core Ops, SparseCore 0:
  231.1 49.8 all-gather.4
  433.2 57.3 all-gather.6
where the time goes:
time: 555 us; the launch traced here: 546 us
  waiting for transfers between devices  209 us (38%)
  blocking collectives  136 us (25%)
  matrix products  57.4 us (10%)
  starting transfers between devices  49.8 us (9%)
  between operations  38.2 us (7%)
  local copies, waits for them, and re-layouts  29 us (5%)
  other arithmetic  26.1 us (5%)
    all_to_all x8, waiting for transfers between devices, copy_for_each(): lax.all_to_all(jnp.broadcast_to(shard[None], (peers, *shard.shape)), axis...  116 us
    all_to_all x5, blocking collectives, copy_for_each(): lax.all_to_all(jnp.broadcast_to(shard[None], (peers, *shard.shape)), axis...  95.3 us
    all_gather x2, waiting for transfers between devices, over_pieces(): pieces = lax.all_gather(shard, axis)  92.5 us
    all_to_all x8, starting transfers between devices, copy_for_each(): lax.all_to_all(jnp.broadcast_to(shard[None], (peers, *shard.shape)), axis...  49.6 us
    pmax x5, blocking collectives, one_axis_at_a_time(): shard = lax.pmax(shard, axis)  41.2 us
    dot_general x14, matrix products, forward(): jnp.einsum('tkab,tkb->ta', blocks, gathered, precision=lax.Precision.HIGH...  25.5 us
    dot_general x15, matrix products, backward(): jnp.einsum('tkab,ta->tkb', blocks, vector_blocks, precision=lax.Precision...  22.8 us
    broadcast_in_dim x13, local copies, waits for them, and re-layouts, copy_for_each(): jnp.broadcast_to(shard[None], (peers, *shard.shape))  11.2 us
  transfers between devices with their start and end apart: 10, of which 9 were waited for; matrix products, arithmetic and copies ran while one was open for 2% of the time, Pallas kernels for 0%

commit v1 on v0

v1 whole, which is shorter than its diff:
```python
import jax
import jax.numpy as jnp
from jax import lax
from jax.experimental import pallas as pl
from jax.experimental.pallas import tpu as pltpu
from jax.sharding import Mesh
from jax.sharding import PartitionSpec as P

BS = 256
LANES = 128
ROW = ("row_0", "row_1", "row_2")
COL = ("col_0", "col_1")
PEERS = 16
VROWS = 128

sigma_shift = 1e-06
rho_step = 0.1
relaxation = 1.6

f32 = jnp.float32
VMEM = pl.BlockSpec(memory_space=pltpu.VMEM)
SMEM = pl.BlockSpec(memory_space=pltpu.SMEM)


def kernel_call(body, name, outs, scratch=()):
    def call(meta, *arrays):
        return pl.pallas_call(
            body,
            name=name,
            out_shape=[jax.ShapeDtypeStruct(s, f32) for s in outs],
            in_specs=[SMEM] + [VMEM] * len(arrays),
            out_specs=[VMEM] * len(outs),
            scratch_shapes=[pltpu.VMEM(s, f32) for s in scratch],
            compiler_params=pltpu.CompilerParams(vmem_limit_bytes=4 << 20),
        )(meta, *arrays)

    return call


def row_sum(a):
    return jnp.sum(a, axis=0, keepdims=True)


def forward(mat, touched, out, at):
    for t in range(4):
        for ha in range(2):
            acc = None
            for k in range(2):
                for lt in range(2):
                    j = 2 * t + lt
                    tile = mat[t, k, ha * LANES : (ha + 1) * LANES, lt * LANES : (lt + 1) * LANES]
                    term = tile * touched[k][j : j + 1, :]
                    acc = term if acc is None else acc + term
            j = at + 2 * t + ha
            out[j : j + 1, :] = row_sum(acc.T)


def backward(pairs, pattern, out, at):
    for t in range(4):
        acc = [[None, None], [None, None]]
        for mat, v in pairs:
            for ha in range(2):
                j = 2 * t + ha
                column = jnp.broadcast_to(v[j : j + 1, :], (LANES, LANES)).T
                for k in range(2):
                    for lt in range(2):
                        tile = mat[t, k, ha * LANES : (ha + 1) * LANES, lt * LANES : (lt + 1) * LANES]
                        part = (tile * column).reshape(16, 8, LANES).sum(axis=0)
                        acc[k][lt] = part if acc[k][lt] is None else acc[k][lt] + part
        for k in range(2):
            for lt in range(2):
                j = 2 * t + lt
                out[at + 8 * k + j : at + 8 * k + j + 1, :] = (
                    row_sum(acc[k][lt]) * pattern[k, j : j + 1, :]
                )


def gather_touched(meta, vector, pattern, ring):
    ring[0:VROWS, :] = vector
    ring[VROWS : VROWS + 8, :] = vector[0:8, :]
    return [ring[pl.ds(meta[2 + k], 8), :] * pattern[k] for k in range(2)]


def assemble(meta, received, at, turn):
    total = None
    for k in range(2):
        for peer in range(PEERS):
            part = received[peer, at + 8 * k : at + 8 * k + 8, :]
            turn[k, 8 * peer : 8 * peer + 8, :] = part
            turn[k, VROWS + 8 * peer : VROWS + 8 * peer + 8, :] = part
        turned = turn[k, pl.ds(meta[k], VROWS), :]
        total = turned if total is None else total + turned
    return total


def to_all(line, out):
    value = line[...]
    for peer in range(PEERS):
        out[peer, :, :] = value


def peer_total(received, lo, hi):
    total = received[0, lo:hi, :]
    for peer in range(1, PEERS):
        total = total + received[peer, lo:hi, :]
    return total


def peer_max(received, lo, hi):
    total = received[0, lo:hi, :]
    for peer in range(1, PEERS):
        total = jnp.maximum(total, received[peer, lo:hi, :])
    return total


def lane_total(a):
    return jnp.sum(a, axis=1, keepdims=True)


def products_of(meta, vector, mats, pattern, ring, line):
    touched = gather_touched(meta, vector, pattern, ring)
    forward(mats[0], touched, line, 0)
    forward(mats[1], touched, line, 8)


def first_products(meta, A, G, pat, x, out, line, ring):
    products_of(meta, x[...], (G, A), pat, ring, line)
    to_all(line, out)


def start_rows(z, y, gx, ax):
    return rho_step * z - y - rho_step * ax, -gx


def first_start(meta, A, G, pat, recv, z, y, out, gx_out, ax_out, line):
    gx = peer_total(recv, 0, 8)
    ax = peer_total(recv, 8, 16)
    gx_out[...] = gx
    ax_out[...] = ax
    va, vg = start_rows(z[...], y[...], gx, ax)
    backward(((A, va), (G, vg)), pat, line, 0)
    to_all(line, out)


def begin_solve(meta, A, G, pat, recv, x, diag, lin, out, rem_out, *rest, dual):
    if dual:
        dual_out, line, ring, turn = rest
    else:
        line, ring, turn = rest
    start = assemble(meta, recv, 0, turn)
    xv = x[...]
    shifted = diag[...] + sigma_shift
    rem = sigma_shift * xv - lin[...] - shifted * xv + start
    rem_out[...] = rem
    products_of(meta, rem, (G, A), pat, ring, line)
    line[16:17, :] = row_sum(rem * rem)
    line[17:18, :] = row_sum(rem * shifted * rem)
    line[18:24, :] = jnp.zeros((6, LANES), f32)
    to_all(line, out)
    if dual:
        residual = diag[...] * xv + lin[...] + assemble(meta, recv, 16, turn)
        dual_out[...] = jnp.max(jnp.abs(residual), axis=0, keepdims=True)


def first_image(meta, A, G, pat, recv, out, gd_out, ad_out, sc_out, line):
    gd = peer_total(recv, 0, 8)
    ad = peer_total(recv, 8, 16)
    gd_out[...] = gd
    ad_out[...] = ad
    sc_out[...] = peer_total(recv, 16, 24)
    backward(((G, gd), (A, rho_step * ad)), pat, line, 0)
    line[16:17, :] = row_sum(gd * gd + rho_step * (ad * ad))
    line[17:24, :] = jnp.zeros((7, LANES), f32)
    to_all(line, out)


def first_step(meta, A, G, pat, recv, direction, sc, diag, out, rem_out, step_out, line, ring, turn):
    image_part = assemble(meta, recv, 0, turn)
    squares = lane_total(peer_total(recv, 16, 24))[0:1, :]
    scalars = lane_total(sc[...])
    norm, weighted = scalars[0:1, :], scalars[1:2, :]
    step = norm / (squares + weighted)
    d = direction[...]
    shifted = diag[...] + sigma_shift
    rem = d - step * (image_part + shifted * d)
    rem_out[...] = rem
    step_out[...] = jnp.broadcast_to(step, (8, LANES))
    products_of(meta, rem, (G, A), pat, ring, line)
    weighted_rem = rem * shifted
    line[16:17, :] = row_sum(rem * rem)
    line[17:18, :] = row_sum(weighted_rem * rem)
    line[18:19, :] = row_sum(weighted_rem * d)
    line[19:24, :] = jnp.zeros((5, LANES), f32)
    to_all(line, out)


def second_images(meta, recv, gd, ad, sc, out, gd_out, ad_out, small_out):
    scalars = lane_total(peer_total(recv, 16, 24))
    norm, weighted_rem, weighted_mix = scalars[0:1, :], scalars[1:2, :], scalars[2:3, :]
    before = lane_total(sc[...])
    norm_old, weighted_old = before[0:1, :], before[1:2, :]
    ratio = norm / norm_old
    gd2 = peer_total(recv, 0, 8) + ratio * gd[...]
    ad2 = peer_total(recv, 8, 16) + ratio * ad[...]
    gd_out[...] = gd2
    ad_out[...] = ad2
    weighted = weighted_rem + 2.0 * ratio * weighted_mix + ratio * ratio * weighted_old
    small_out[0:1, :] = jnp.broadcast_to(norm, (1, LANES))
    small_out[1:2, :] = jnp.broadcast_to(weighted, (1, LANES))
    small_out[2:3, :] = jnp.broadcast_to(ratio, (1, LANES))
    small_out[3:8, :] = jnp.zeros((5, LANES), f32)
    squares = gd2 * gd2 + rho_step * (ad2 * ad2)
    for peer in range(PEERS):
        out[peer, :, :] = squares


def update(
    meta, A, G, pat, recv, small, step, gd, ad, gd2, ad2, gx, ax, x, rem, d, z, y, lo, hi,
    *rest, last,
):
    if last:
        primal0, out, x_out, z_out, y_out, line = rest
    else:
        out, x_out, z_out, y_out, gx_out, ax_out, primal_out, line = rest
    squares = lane_total(row_sum(peer_total(recv, 0, 8)))
    sm = small[...]
    norm, weighted, ratio = sm[0:1, :], sm[1:2, :], sm[2:3, :]
    step2 = norm / (squares + weighted)
    step1 = step[0:1, :]
    dv = d[...]
    xv = x[...]
    solved = xv + step1 * dv + step2 * (rem[...] + ratio * dv)
    x_out[...] = relaxation * solved + (1.0 - relaxation) * xv
    axv = ax[...]
    tracked = axv + step1 * ad[...] + step2 * ad2[...]
    zv, yv = z[...], y[...]
    blended = relaxation * tracked + (1.0 - relaxation) * zv
    z_new = jnp.minimum(jnp.maximum(blended + yv / rho_step, lo[...]), hi[...])
    y_new = yv + rho_step * (blended - z_new)
    z_out[...] = z_new
    y_out[...] = y_new
    gxv = gx[...]
    gx_new = relaxation * (gxv + step1 * gd[...] + step2 * gd2[...]) + (1.0 - relaxation) * gxv
    ax_new = relaxation * tracked + (1.0 - relaxation) * axv
    primal = jnp.max(jnp.abs(ax_new - z_new), axis=0, keepdims=True)
    if last:
        backward(((G, gx_new), (A, y_new)), pat, line, 0)
        line[16:17, :] = primal0[...]
        line[17:18, :] = primal
        line[18:24, :] = jnp.zeros((6, LANES), f32)
    else:
        gx_out[...] = gx_new
        ax_out[...] = ax_new
        primal_out[...] = primal
        va, vg = start_rows(z_new, y_new, gx_new, ax_new)
        backward(((A, va), (G, vg)), pat, line, 0)
        backward(((G, gx_new), (A, y_new)), pat, line, 16)
    to_all(line, out)


def last_dual(meta, recv, x, diag, lin, dual0, out, turn):
    residual = diag[...] * x[...] + lin[...] + assemble(meta, recv, 0, turn)
    primal = peer_max(recv, 16, 24)
    dual = jnp.max(jnp.abs(residual), axis=0, keepdims=True)
    value = jnp.concatenate([primal[0:2, :], dual0[...], dual, jnp.zeros((4, LANES), f32)], axis=0)
    for peer in range(PEERS):
        out[peer, :, :] = value


def finish(meta, recv, out):
    top = jnp.max(peer_max(recv, 0, 8), axis=1, keepdims=True)
    out[0:1, 0:1] = top[0:1, :]
    out[0:1, 1:2] = top[1:2, :]
    out[1:2, 0:1] = top[2:3, :]
    out[1:2, 1:2] = top[3:4, :]


V = (VROWS, LANES)
R8 = (8, LANES)
ONE = (1, LANES)
RING = (VROWS + 8, LANES)
TURN = (2, 2 * VROWS, LANES)


def payload(rows):
    return (PEERS, rows, LANES)


def exchange(a, axes):
    return lax.all_to_all(a, axes, 0, 0, tiled=True)


def local(
    constraint_blocks, factor_blocks, band_offsets, block_pattern, cost_linear, cost_diagonal,
    lower, upper, x_start, z_start, y_start,
):
    A, G = constraint_blocks, factor_blocks
    offsets = band_offsets[0]
    first_row = lax.axis_index(ROW) * 4
    meta = jnp.concatenate([VROWS - 2 * offsets, 2 * ((first_row + offsets) % 64)])
    pat = jnp.broadcast_to(
        block_pattern.astype(f32).T[:, :, None, None], (2, 4, 2, LANES)
    ).reshape(2, 8, LANES)
    lin, diag = cost_linear.reshape(V), cost_diagonal.reshape(V)
    lo, hi = lower.reshape(R8), upper.reshape(R8)
    x, z, y = x_start.reshape(V), z_start.reshape(R8), y_start.reshape(R8)

    (out,) = kernel_call(first_products, "first_products", [payload(16)], [(16, LANES), RING])(
        meta, A, G, pat, x
    )
    recv = exchange(out, COL)
    out, gx, ax = kernel_call(first_start, "first_start", [payload(16), R8, R8], [(16, LANES)])(
        meta, A, G, pat, recv, z, y
    )
    primal0 = dual0 = None
    for outer in range(2):
        recv = exchange(out, ROW)
        shapes = [payload(24), V] + ([ONE] if outer else [])

        def body(*refs, dual=bool(outer)):
            begin_solve(*refs, dual=dual)

        got = kernel_call(body, f"begin_solve_{outer}", shapes, [(24, LANES), RING, TURN])(
            meta, A, G, pat, recv, x, diag, lin
        )
        out, d = got[:2]
        if outer:
            dual0 = got[2]
        recv = exchange(out, COL)
        out, gd, ad, sc = kernel_call(
            first_image, "first_image", [payload(24), R8, R8, R8], [(24, LANES)]
        )(meta, A, G, pat, recv)
        recv = exchange(out, ROW)
        out, rem, step = kernel_call(
            first_step, "first_step", [payload(24), V, R8], [(24, LANES), RING, TURN]
        )(meta, A, G, pat, recv, d, sc, diag)
        recv = exchange(out, COL)
        out, gd2, ad2, small = kernel_call(second_images, "second_images", [payload(8), R8, R8, R8])(
            meta, recv, gd, ad, sc
        )
        recv = exchange(out, ROW)
        args = (meta, A, G, pat, recv, small, step, gd, ad, gd2, ad2, gx, ax, x, rem, d, z, y, lo, hi)
        if outer == 0:

            def body(*refs):
                update(*refs, last=False)

            out, x, z, y, gx, ax, primal0 = kernel_call(
                body, "update_0", [payload(32), V, R8, R8, R8, R8, ONE], [(32, LANES)]
            )(*args)
        else:

            def body(*refs):
                update(*refs, last=True)

            out, x, z, y = kernel_call(body, "update_1", [payload(24), V, R8, R8], [(24, LANES)])(
                *args, primal0
            )
    recv = exchange(out, ROW)
    (out,) = kernel_call(last_dual, "last_dual", [payload(8)], [TURN])(meta, recv, x, diag, lin, dual0)
    recv = exchange(out, COL)
    (residuals,) = kernel_call(finish, "finish", [(2, 2)])(meta, recv)
    return x.reshape(-1), z.reshape(-1), y.reshape(-1), residuals


def solution(mesh):
    torus = Mesh(mesh.devices.reshape(2, 4, 2, 4, 4), ROW + COL)
    in_specs = (
        P(ROW, COL, None, None), P(ROW, COL, None, None), P(COL, None), P(ROW, COL), P(COL), P(COL),
        P(ROW), P(ROW), P(COL), P(ROW), P(ROW),
    )
    out_specs = (P(COL), P(ROW), P(ROW), P())
    return jax.shard_map(local, mesh=torus, in_specs=in_specs, out_specs=out_specs, check_vma=False)
```

time: 555 us -> 208 us (0.37); the launches traced: 546 us -> 207 us
  waiting for transfers between devices: 209 us -> 0 us
  matrix products: 57.4 us -> 0 us
  blocking collectives: 136 us -> 186 us
  starting transfers between devices: 49.8 us -> 0 us
  between operations: 38.2 us -> 0.71 us
  other arithmetic: 26.1 us -> 2.08 us
  local copies, waits for them, and re-layouts: 29 us -> 5.12 us
  Pallas kernels: 0 us -> 13.7 us
    all_to_all x8 -> x0, waiting for transfers between devices: 116 us -> none  [copy_for_each(): lax.all_to_all(jnp.broadcast_to(shard[None], (peers, *shard.shape)), axis...]
    all_gather x2 -> x0, waiting for transfers between devices: 92.5 us -> none  [over_pieces(): pieces = lax.all_gather(shard, axis)]
    all_to_all x5 -> x13, blocking collectives: 95.3 us -> 186 us  [exchange(): return lax.all_to_all(a, axes, 0, 0, tiled=True)]
    dot_general x51 -> x0, matrix products: 57.4 us -> none  [the longest x14 25.5 us: forward(): jnp.einsum('tkab,tkb->ta', blocks, gathered, precision=lax.Precision.HIGH...]
    all_to_all x8 -> x0, starting transfers between devices: 49.6 us -> none  [copy_for_each(): lax.all_to_all(jnp.broadcast_to(shard[None], (peers, *shard.shape)), axis...]
    pmax x5 -> x0, blocking collectives: 41.2 us -> none  [one_axis_at_a_time(): shard = lax.pmax(shard, axis)]
    reduce_sum x23 -> x0, other arithmetic: 16.9 us -> none  [the longest x13 6.18 us: taken_together(): return jnp.sum(everything, axis=0)]
    pallas_call x0 -> x14, Pallas kernels: none -> 13.7 us  [call(): pl.pallas_call(body, name=name, out_shape=[jax.ShapeDtypeStruct(s, f32) f...]
  transfers between devices with their start and end apart: 10 -> 0, of which waited for: 9 -> 0; matrix products, arithmetic and copies ran while one was open for 2% -> 0% of each run, Pallas kernels for 0% -> 0%
where the time goes in v1:
time: 208 us; the launch traced here: 207 us
  blocking collectives  186 us (89%)
  Pallas kernels  13.7 us (7%)
  local copies, waits for them, and re-layouts  5.12 us (2%)
  other arithmetic  2.08 us (1%)
    all_to_all x13, blocking collectives, exchange(): return lax.all_to_all(a, axes, 0, 0, tiled=True)  186 us
    pallas_call x14, Pallas kernels, call(): pl.pallas_call(body, name=name, out_shape=[jax.ShapeDtypeStruct(s, f32) f...  13.7 us
    unnamed x24, local copies, waits for them, and re-layouts  4.9 us

profile of v1, /device:TPU:2, one launch (start us, length us, event | category | flops | bytes accessed | tf_op | source)
XLA Modules:
  0.0 207.4 jit_solution(3021148401733741656)
XLA Ops:
  0.6 0.7 subtract_bitcast_fusion
  1.3 0.7 fusion
  2.0 0.7 convert_bitcast_fusion
  2.6 0.1 broadcast_in_dim.10
  2.7 0.1 broadcast_in_dim.11
  2.8 0.1 pad_add_fusion.meta.refs_0_
  2.9 0.1 broadcast_in_dim.12.pat.refs_3_
  2.9 0.0 copy-start
  3.0 1.6 copy-done
  4.5 1.6 copy-done.2
  6.1 0.8 copy-done.4
  7.0 0.9 first_products.1
  7.9 15.7 %all_to_all.65.recv = f32[16,16,128]{2,1,0:T(8,128)S(1)} all-to-all(f32[16,16,128]{2,1,0:T(8,128)S(1)} %first_products.1), channel_id=1, replica_groups=mesh['row_0'=2,'row_1'=4,'row_2'=2,'col_0'=4,'col_1'=4] {'col_0','col_1'}, dimensions={0} | all-to-all | bytes 262144 | tf_op jit(solution)/shard_map/all_to_all | solution.py:290
  23.6 0.0 copy-done.8
  23.6 0.0 copy-done.9
  23.6 0.0 copy-start.6
  23.7 0.9 first_start.1
  24.6 18.9 %all_to_all.66.refs_4_ = f32[16,16,128]{2,1,0:T(8,128)S(1)} all-to-all(f32[16,16,128]{2,1,0:T(8,128)S(1)} %get-tuple-element.45), channel_id=1, replica_groups=mesh['row_0'=2,'row_1'=4,'row_2'=2,'col_0'=4,'col_1'=4] {'row_0','row_1'..., dimensions={0} | all-to-all | bytes 262144 | tf_op jit(solution)/shard_map/all_to_all | solution.py:290
  43.5 0.0 copy-done.3
  43.5 0.0 copy-done.5
  43.5 0.0 copy-done.6
  43.5 1.0 begin_solve_0.1
  44.5 12.5 %all_to_all.67.recv = f32[16,24,128]{2,1,0:T(8,128)S(1)} all-to-all(f32[16,24,128]{2,1,0:T(8,128)S(1)} %get-tuple-element.46), channel_id=1, replica_groups=mesh['row_0'=2,'row_1'=4,'row_2'=2,'col_0'=4,'col_1'=4] {'col_0','col_1'}, dimensions={0} | all-to-all | bytes 393216 | tf_op jit(solution)/shard_map/all_to_all | solution.py:290
  57.0 0.9 first_image.2
  57.9 14.0 %all_to_all.68.recv = f32[16,24,128]{2,1,0:T(8,128)S(1)} all-to-all(f32[16,24,128]{2,1,0:T(8,128)S(1)} %get-tuple-element.47), channel_id=1, replica_groups=mesh['row_0'=2,'row_1'=4,'row_2'=2,'col_0'=4,'col_1'=4] {'row_0','row_1'..., dimensions={0} | all-to-all | bytes 393216 | tf_op jit(solution)/shard_map/all_to_all | solution.py:290
  71.9 1.1 first_step.2
  73.0 13.8 %all_to_all.69.recv = f32[16,24,128]{2,1,0:T(8,128)S(1)} all-to-all(f32[16,24,128]{2,1,0:T(8,128)S(1)} %get-tuple-element.50), channel_id=1, replica_groups=mesh['row_0'=2,'row_1'=4,'row_2'=2,'col_0'=4,'col_1'=4] {'col_0','col_1'}, dimensions={0} | all-to-all | bytes 393216 | tf_op jit(solution)/shard_map/all_to_all | solution.py:290
  86.8 0.7 second_images.2
  87.5 12.8 %all_to_all.70.refs_4_ = f32[16,8,128]{2,1,0:T(8,128)S(1)} all-to-all(f32[16,8,128]{2,1,0:T(8,128)S(1)} %get-tuple-element.53), channel_id=1, replica_groups=mesh['row_0'=2,'row_1'=4,'row_2'=2,'col_0'=4,'col_1'=4] {'row_0','row_1'..., dimensions={0} | all-to-all | bytes 131072 | tf_op jit(solution)/shard_map/all_to_all | solution.py:290
  100.3 0.0 copy-done.1
  100.3 0.0 copy-done.10
  100.3 0.0 copy-done.11
  100.3 1.4 update_0.1
  101.7 14.7 %all_to_all.71.refs_4_ = f32[16,32,128]{2,1,0:T(8,128)S(1)} all-to-all(f32[16,32,128]{2,1,0:T(8,128)S(1)} %get-tuple-element.61), channel_id=1, replica_groups=mesh['row_0'=2,'row_1'=4,'row_2'=2,'col_0'=4,'col_1'=4] {'row_0','row_1'..., dimensions={0} | all-to-all | bytes 524288 | tf_op jit(solution)/shard_map/all_to_all | solution.py:290
  116.4 1.0 begin_solve_1.1
  117.4 14.9 %all_to_all.72.recv = f32[16,24,128]{2,1,0:T(8,128)S(1)} all-to-all(f32[16,24,128]{2,1,0:T(8,128)S(1)} %get-tuple-element.63), channel_id=1, replica_groups=mesh['row_0'=2,'row_1'=4,'row_2'=2,'col_0'=4,'col_1'=4] {'col_0','col_1'}, dimensions={0} | all-to-all | bytes 393216 | tf_op jit(solution)/shard_map/all_to_all | solution.py:290
  132.3 0.9 first_image.3
  133.2 14.2 %all_to_all.73.recv = f32[16,24,128]{2,1,0:T(8,128)S(1)} all-to-all(f32[16,24,128]{2,1,0:T(8,128)S(1)} %get-tuple-element.64), channel_id=1, replica_groups=mesh['row_0'=2,'row_1'=4,'row_2'=2,'col_0'=4,'col_1'=4] {'row_0','row_1'..., dimensions={0} | all-to-all | bytes 393216 | tf_op jit(solution)/shard_map/all_to_all | solution.py:290
  147.4 1.1 first_step.3
  148.5 13.9 %all_to_all.74.recv = f32[16,24,128]{2,1,0:T(8,128)S(1)} all-to-all(f32[16,24,128]{2,1,0:T(8,128)S(1)} %get-tuple-element.67), channel_id=1, replica_groups=mesh['row_0'=2,'row_1'=4,'row_2'=2,'col_0'=4,'col_1'=4] {'col_0','col_1'}, dimensions={0} | all-to-all | bytes 393216 | tf_op jit(solution)/shard_map/all_to_all | solution.py:290
  162.4 0.7 second_images.3
  163.1 12.8 %all_to_all.75.refs_4_ = f32[16,8,128]{2,1,0:T(8,128)S(1)} all-to-all(f32[16,8,128]{2,1,0:T(8,128)S(1)} %get-tuple-element.70), channel_id=1, replica_groups=mesh['row_0'=2,'row_1'=4,'row_2'=2,'col_0'=4,'col_1'=4] {'row_0','row_1'..., dimensions={0} | all-to-all | bytes 131072 | tf_op jit(solution)/shard_map/all_to_all | solution.py:290
  175.9 1.3 update_1.1
  177.2 14.0 %all_to_all.76.recv = f32[16,24,128]{2,1,0:T(8,128)S(1)} all-to-all(f32[16,24,128]{2,1,0:T(8,128)S(1)} %get-tuple-element.84), channel_id=1, replica_groups=mesh['row_0'=2,'row_1'=4,'row_2'=2,'col_0'=4,'col_1'=4] {'row_0','row_1'..., dimensions={0} | all-to-all | bytes 393216 | tf_op jit(solution)/shard_map/all_to_all | solution.py:290
  191.2 0.8 copy-done.7
  192.0 0.6 last_dual.1
  192.6 13.6 %all_to_all.77.recv = f32[16,8,128]{2,1,0:T(8,128)S(1)} all-to-all(f32[16,8,128]{2,1,0:T(8,128)S(1)} %last_dual.1), channel_id=1, replica_groups=mesh['row_0'=2,'row_1'=4,'row_2'=2,'col_0'=4,'col_1'=4] {'col_0','col_1'}, dimensions={0} | all-to-all | bytes 131072 | tf_op jit(solution)/shard_map/all_to_all | solution.py:290
  206.2 1.2 finish.1
  (10 shorter events, 0.0 us)
Async XLA Ops:
  2.9 1.6 copy-start
  4.5 1.6 copy-start.2
  6.1 0.8 copy-start.4
  7.0 16.7 %copy-start.8 = (f32[1024]{0:T(1024)S(1)}, f32[1024]{0:T(1024)}, u32[]{:S(2)}) copy-start(f32[1024]{0:T(1024)} %param.20) | copy-start | bytes 12292
  7.0 16.7 %copy-start.9 = (f32[1024]{0:T(1024)S(1)}, f32[1024]{0:T(1024)}, u32[]{:S(2)}) copy-start(f32[1024]{0:T(1024)} %param.21) | copy-start | bytes 12292
  23.6 19.8 %copy-start.3 = (f32[16384]{0:T(1024)S(1)}, f32[16384]{0:T(1024)}, u32[]{:S(2)}) copy-start(f32[16384]{0:T(1024)} %param.16) | copy-start | bytes 196612
  23.6 19.8 %copy-start.5 = (f32[16384]{0:T(1024)S(1)}, f32[16384]{0:T(1024)}, u32[]{:S(2)}) copy-start(f32[16384]{0:T(1024)} %param.19) | copy-start | bytes 196612
  23.6 19.8 %copy-start.6 = (f32[16384]{0:T(1024)S(1)}, f32[16384]{0:T(1024)}, u32[]{:S(2)}) copy-start(f32[16384]{0:T(1024)} %param.15) | copy-start | bytes 196612
  71.9 28.4 %copy-start.1 = (f32[4,2,256,256]{3,2,1,0:T(8,128)S(1)}, f32[4,2,256,256]{3,2,1,0:T(8,128)}, u32[]{:S(2)}) copy-start(f32[4,2,256,256]{3,2,1,0:T(8,128)} %refs_1_.7) | copy-start | bytes 6291460
  71.9 28.4 %copy-start.10 = (f32[1024]{0:T(1024)S(1)}, f32[1024]{0:T(1024)}, u32[]{:S(2)}) copy-start(f32[1024]{0:T(1024)} %param.17) | copy-start | bytes 12292
  71.9 28.4 %copy-start.11 = (f32[1024]{0:T(1024)S(1)}, f32[1024]{0:T(1024)}, u32[]{:S(2)}) copy-start(f32[1024]{0:T(1024)} %param.18) | copy-start | bytes 12292
  191.2 0.8 copy-start.7

commit v2 on v1

v2 whole, which is shorter than its diff:
```python
import jax
import jax.numpy as jnp
from jax import lax
from jax.experimental import pallas as pl
from jax.experimental.pallas import tpu as pltpu
from jax.sharding import Mesh
from jax.sharding import PartitionSpec as P

BS = 256
LANES = 128
ROW = ("row_0", "row_1", "row_2")
COL = ("col_0", "col_1")
PEERS = 16
VROWS = 128

sigma_shift = 1e-06
rho_step = 0.1
relaxation = 1.6

f32 = jnp.float32
VMEM = pl.BlockSpec(memory_space=pltpu.VMEM)
SMEM = pl.BlockSpec(memory_space=pltpu.SMEM)


def kernel_call(body, name, outs, scratch=(), spaces=None):
    def call(*arrays):
        return pl.pallas_call(
            body,
            name=name,
            out_shape=[jax.ShapeDtypeStruct(s, f32) for s in outs],
            in_specs=spaces or [SMEM] + [VMEM] * (len(arrays) - 1),
            out_specs=[VMEM] * len(outs),
            scratch_shapes=[pltpu.VMEM(s, f32) if isinstance(s, tuple) else s for s in scratch],
            compiler_params=pltpu.CompilerParams(vmem_limit_bytes=8 << 20),
        )(*arrays)

    return call


def row_sum(a):
    return jnp.sum(a, axis=0, keepdims=True)


def forward_row(mat, t, touched, out, at):
    for ha in range(2):
        acc = None
        for k in range(2):
            for lt in range(2):
                j = 2 * t + lt
                tile = mat[t, k, ha * LANES : (ha + 1) * LANES, lt * LANES : (lt + 1) * LANES]
                term = tile * touched[k][j : j + 1, :]
                acc = term if acc is None else acc + term
        j = at + 2 * t + ha
        out[j : j + 1, :] = row_sum(acc.T)


def forward(mat, touched, out, at):
    for t in range(4):
        forward_row(mat, t, touched, out, at)


def backward(pairs, pattern, out, at):
    for t in range(4):
        acc = [[None, None], [None, None]]
        for mat, v in pairs:
            for ha in range(2):
                j = 2 * t + ha
                column = jnp.broadcast_to(v[j : j + 1, :], (LANES, LANES)).T
                for k in range(2):
                    for lt in range(2):
                        tile = mat[t, k, ha * LANES : (ha + 1) * LANES, lt * LANES : (lt + 1) * LANES]
                        part = (tile * column).reshape(16, 8, LANES).sum(axis=0)
                        acc[k][lt] = part if acc[k][lt] is None else acc[k][lt] + part
        for k in range(2):
            for lt in range(2):
                j = 2 * t + lt
                out[at + 8 * k + j : at + 8 * k + j + 1, :] = (
                    row_sum(acc[k][lt]) * pattern[k, j : j + 1, :]
                )


def first_touched(offsets, k):
    return 2 * ((lax.axis_index(ROW) * 4 + offsets[0, k]) % 64)


def gather_touched(offsets, vector, pattern, ring):
    ring[0:VROWS, :] = vector
    ring[VROWS : VROWS + 8, :] = vector[0:8, :]
    return [ring[pl.ds(first_touched(offsets, k), 8), :] * pattern[k] for k in range(2)]


def assemble(offsets, received, each, at, turn):
    total = None
    for k in range(2):
        for peer in range(PEERS):
            lo = each * peer + at + 8 * k
            part = received[lo : lo + 8, :]
            turn[k, 8 * peer : 8 * peer + 8, :] = part
            turn[k, VROWS + 8 * peer : VROWS + 8 * peer + 8, :] = part
        turned = turn[k, pl.ds(VROWS - 2 * offsets[0, k], VROWS), :]
        total = turned if total is None else total + turned
    return total


def to_all(line, out):
    each = out.shape[0] // PEERS
    value = line[0:each, :]
    for peer in range(PEERS):
        out[each * peer : each * (peer + 1), :] = value


def peer_total(received, each, lo, hi):
    total = received[lo:hi, :]
    for peer in range(1, PEERS):
        total = total + received[each * peer + lo : each * peer + hi, :]
    return total


def lane_total(a):
    return jnp.sum(a, axis=1, keepdims=True)


def full_total(a):
    return lane_total(row_sum(a))


def full_max(a):
    return jnp.max(jnp.max(a, axis=0, keepdims=True), axis=1, keepdims=True)


def packed(values):
    lane = lax.broadcasted_iota(jnp.int32, (1, LANES), 1)
    row = jnp.zeros((1, LANES), f32)
    for n, value in enumerate(values):
        row = jnp.where(lane == n, value, row)
    return row


def products_of(offsets, vector, mats, pattern, ring, line):
    touched = gather_touched(offsets, vector, pattern, ring)
    forward(mats[0], touched, line, 0)
    forward(mats[1], touched, line, 8)


def first_products(
    offsets_in, pattern_in, A_in, G_in, x_in, out, pat_out, A, G,
    offsets, pattern, line, ring, small_sems, sems,
):
    small = [
        pltpu.make_async_copy(offsets_in, offsets, small_sems.at[0]),
        pltpu.make_async_copy(pattern_in, pattern, small_sems.at[1]),
        pltpu.make_async_copy(x_in, ring.at[0:VROWS, :], small_sems.at[2]),
        pltpu.make_async_copy(x_in.at[0:8, :], ring.at[VROWS : VROWS + 8, :], small_sems.at[3]),
    ]
    big = [
        [pltpu.make_async_copy(src.at[t], dst.at[t], sems.at[m, t]) for t in range(4)]
        for m, (src, dst) in enumerate(((G_in, G), (A_in, A)))
    ]
    for copy in small + big[0] + big[1]:
        copy.start()
    for copy in small:
        copy.wait()
    for k in range(2):
        for t in range(4):
            pat_out[k, 2 * t : 2 * t + 2, :] = jnp.full((2, LANES), pattern[k, t].astype(f32))
    touched = [ring[pl.ds(first_touched(offsets, k), 8), :] * pat_out[k] for k in range(2)]
    for m, mat in enumerate((G, A)):
        for t in range(4):
            big[m][t].wait()
            forward_row(mat, t, touched, line, 8 * m)
    to_all(line, out)


def start_rows(z, y, gx, ax):
    return rho_step * z - y - rho_step * ax, -gx


def first_start(offsets, A, G, pat, recv, z, y, out, gx_out, ax_out, line):
    gx = peer_total(recv, 16, 0, 8)
    ax = peer_total(recv, 16, 8, 16)
    gx_out[...] = gx
    ax_out[...] = ax
    va, vg = start_rows(z[...], y[...], gx, ax)
    backward(((A, va), (G, vg)), pat, line, 0)
    to_all(line, out)


def begin_solve(offsets, A, G, pat, recv, x, diag, lin, out, rem_out, *rest, dual):
    if dual:
        dual_out, line, ring, turn = rest
    else:
        line, ring, turn = rest
    each = 32 if dual else 16
    start = assemble(offsets, recv, each, 0, turn)
    xv = x[...]
    shifted = diag[...] + sigma_shift
    rem = sigma_shift * xv - lin[...] - shifted * xv + start
    rem_out[...] = rem
    products_of(offsets, rem, (G, A), pat, ring, line)
    line[16:17, :] = packed((full_total(rem * rem), full_total(rem * shifted * rem)))
    to_all(line, out)
    if dual:
        residual = diag[...] * xv + lin[...] + assemble(offsets, recv, each, 16, turn)
        dual_out[...] = jnp.max(jnp.abs(residual), axis=0, keepdims=True)


def first_image(offsets, A, G, pat, recv, out, gd_out, ad_out, sc_out, line):
    gd = peer_total(recv, 17, 0, 8)
    ad = peer_total(recv, 17, 8, 16)
    gd_out[...] = gd
    ad_out[...] = ad
    sc_out[...] = peer_total(recv, 17, 16, 17)
    backward(((G, gd), (A, rho_step * ad)), pat, line, 0)
    line[16:17, :] = row_sum(gd * gd + rho_step * (ad * ad))
    to_all(line, out)


def first_step(
    offsets, A, G, pat, recv, direction, sc, diag, out, rem_out, step_out, line, ring, turn
):
    image_part = assemble(offsets, recv, 17, 0, turn)
    squares = lane_total(peer_total(recv, 17, 16, 17))
    norm, weighted = sc[0:1, 0:1], sc[0:1, 1:2]
    step = norm / (squares + weighted)
    d = direction[...]
    shifted = diag[...] + sigma_shift
    rem = d - step * (image_part + shifted * d)
    rem_out[...] = rem
    step_out[...] = jnp.broadcast_to(step, (1, LANES))
    products_of(offsets, rem, (G, A), pat, ring, line)
    weighted_rem = rem * shifted
    line[16:17, :] = packed(
        (full_total(rem * rem), full_total(weighted_rem * rem), full_total(weighted_rem * d))
    )
    to_all(line, out)


def second_images(offsets, recv, gd, ad, sc, out, gd_out, ad_out, small_out):
    now = peer_total(recv, 17, 16, 17)
    norm, weighted_rem, weighted_mix = now[:, 0:1], now[:, 1:2], now[:, 2:3]
    norm_old, weighted_old = sc[0:1, 0:1], sc[0:1, 1:2]
    ratio = norm / norm_old
    gd2 = peer_total(recv, 17, 0, 8) + ratio * gd[...]
    ad2 = peer_total(recv, 17, 8, 16) + ratio * ad[...]
    gd_out[...] = gd2
    ad_out[...] = ad2
    weighted = weighted_rem + 2.0 * ratio * weighted_mix + ratio * ratio * weighted_old
    small_out[...] = packed((norm, weighted, ratio))
    squares = row_sum(gd2 * gd2 + rho_step * (ad2 * ad2))
    out[...] = jnp.broadcast_to(squares, (PEERS, LANES))


def update(
    offsets, A, G, pat, recv, small, step, gd, ad, gd2, ad2, gx, ax, x, rem, d, z, y, lo, hi,
    *rest, last,
):
    if last:
        diag, lin, primal0, out, x_out, z_out, y_out, base_out, line = rest
    else:
        out, x_out, z_out, y_out, gx_out, ax_out, primal_out, line = rest
    squares = full_total(recv[...])
    norm, weighted, ratio = small[0:1, 0:1], small[0:1, 1:2], small[0:1, 2:3]
    step2 = norm / (squares + weighted)
    step1 = step[0:1, :]
    axv = ax[...]
    tracked = axv + step1 * ad[...] + step2 * ad2[...]
    zv, yv = z[...], y[...]
    blended = relaxation * tracked + (1.0 - relaxation) * zv
    z_new = jnp.minimum(jnp.maximum(blended + yv / rho_step, lo[...]), hi[...])
    y_new = yv + rho_step * (blended - z_new)
    z_out[...] = z_new
    y_out[...] = y_new
    gxv = gx[...]
    gx_new = relaxation * (gxv + step1 * gd[...] + step2 * gd2[...]) + (1.0 - relaxation) * gxv
    ax_new = relaxation * tracked + (1.0 - relaxation) * axv
    primal = full_max(jnp.abs(ax_new - z_new))
    if last:
        backward(((G, gx_new), (A, y_new)), pat, line, 0)
        line[16:17, :] = packed((primal0[0:1, 0:1], primal))
    else:
        gx_out[...] = gx_new
        ax_out[...] = ax_new
        primal_out[...] = jnp.broadcast_to(primal, (1, LANES))
        va, vg = start_rows(z_new, y_new, gx_new, ax_new)
        backward(((A, va), (G, vg)), pat, line, 0)
        backward(((G, gx_new), (A, y_new)), pat, line, 16)
    to_all(line, out)
    dv = d[...]
    xv = x[...]
    solved = xv + step1 * dv + step2 * (rem[...] + ratio * dv)
    x_new = relaxation * solved + (1.0 - relaxation) * xv
    x_out[...] = x_new
    if last:
        base_out[...] = diag[...] * x_new + lin[...]


def last_dual(offsets, recv, base, dual0, out, turn):
    residual = base[...] + assemble(offsets, recv, 17, 0, turn)
    primal = recv[16:17, :]
    for peer in range(1, PEERS):
        primal = jnp.maximum(primal, recv[17 * peer + 16 : 17 * peer + 17, :])
    row = packed(
        (primal[:, 0:1], primal[:, 1:2], full_max(dual0[...]), full_max(jnp.abs(residual)))
    )
    out[...] = jnp.broadcast_to(row, (PEERS, LANES))


def finish(recv, x, z, y, x_out, z_out, y_out, out):
    x_out[...] = x[...]
    z_out[...] = z[...]
    y_out[...] = y[...]
    top = jnp.max(recv[...], axis=0, keepdims=True)
    out[0:1, :] = top[:, 0:2]
    out[1:2, :] = top[:, 2:4]


V = (VROWS, LANES)
R8 = (8, LANES)
ONE = (1, LANES)
RING = (VROWS + 8, LANES)
TURN = (2, 2 * VROWS, LANES)
BLOCKS = (4, 2, BS, BS)


def payload(rows):
    return (PEERS * rows, LANES)


def exchange(a, axes):
    wide = a.reshape(PEERS, 1, -1)
    return lax.all_to_all(wide, axes, 0, 0, tiled=True).reshape(a.shape)


def local(
    constraint_blocks, factor_blocks, band_offsets, block_pattern, cost_linear, cost_diagonal,
    lower, upper, x_start, z_start, y_start,
):
    A, G, offsets = constraint_blocks, factor_blocks, band_offsets
    lin, diag = cost_linear.reshape(V), cost_diagonal.reshape(V)
    lo, hi = lower.reshape(R8), upper.reshape(R8)
    x, z, y = x_start.reshape(V), z_start.reshape(R8), y_start.reshape(R8)

    out, pat, A, G = kernel_call(
        first_products, "first_products", [payload(16), (2, 8, LANES), BLOCKS, BLOCKS],
        [
            pltpu.SMEM((1, 2), jnp.int32), pltpu.SMEM((2, 4), jnp.int32), (16, LANES), RING,
            pltpu.SemaphoreType.DMA((4,)), pltpu.SemaphoreType.DMA((2, 4)),
        ],
        [pl.BlockSpec(memory_space=pltpu.HBM)] * 5,
    )(*[pltpu.with_memory_space_constraint(a, pltpu.HBM) for a in (offsets, block_pattern.T, A, G, x)])
    recv = exchange(out, COL)
    out, gx, ax = kernel_call(first_start, "first_start", [payload(16), R8, R8], [(16, LANES)])(
        offsets, A, G, pat, recv, z, y
    )
    primal0 = dual0 = None
    for outer in range(2):
        recv = exchange(out, ROW)
        shapes = [payload(17), V] + ([ONE] if outer else [])

        def body(*refs, dual=bool(outer)):
            begin_solve(*refs, dual=dual)

        got = kernel_call(body, f"begin_solve_{outer}", shapes, [(24, LANES), RING, TURN])(
            offsets, A, G, pat, recv, x, diag, lin
        )
        out, d = got[:2]
        if outer:
            dual0 = got[2]
        recv = exchange(out, COL)
        out, gd, ad, sc = kernel_call(
            first_image, "first_image", [payload(17), R8, R8, ONE], [(24, LANES)]
        )(offsets, A, G, pat, recv)
        recv = exchange(out, ROW)
        out, rem, step = kernel_call(
            first_step, "first_step", [payload(17), V, ONE], [(24, LANES), RING, TURN]
        )(offsets, A, G, pat, recv, d, sc, diag)
        recv = exchange(out, COL)
        out, gd2, ad2, small = kernel_call(second_images, "second_images", [payload(1), R8, R8, ONE])(
            offsets, recv, gd, ad, sc
        )
        recv = exchange(out, ROW)
        args = (offsets, A, G, pat, recv, small, step, gd, ad, gd2, ad2, gx, ax, x, rem, d, z, y, lo, hi)
        if outer == 0:

            def body(*refs):
                update(*refs, last=False)

            out, x, z, y, gx, ax, primal0 = kernel_call(
                body, "update_0", [payload(32), V, R8, R8, R8, R8, ONE], [(32, LANES)]
            )(*args)
        else:

            def body(*refs):
                update(*refs, last=True)

            out, x, z, y, base = kernel_call(
                body, "update_1", [payload(17), V, R8, R8, V], [(24, LANES)]
            )(*args, diag, lin, primal0)
    recv = exchange(out, ROW)
    (out,) = kernel_call(last_dual, "last_dual", [payload(1)], [TURN])(offsets, recv, base, dual0)
    recv = exchange(out, COL)
    x, z, y, residuals = kernel_call(finish, "finish", [V, R8, R8, (2, 2)], (), [VMEM] * 4)(recv, x, z, y)
    return x.reshape(-1), z.reshape(-1), y.reshape(-1), residuals


def solution(mesh):
    torus = Mesh(mesh.devices.reshape(2, 4, 2, 4, 4), ROW + COL)
    in_specs = (
        P(ROW, COL, None, None), P(ROW, COL, None, None), P(COL, None), P(ROW, COL), P(COL), P(COL),
        P(ROW), P(ROW), P(COL), P(ROW), P(ROW),
    )
    out_specs = (P(COL), P(ROW), P(ROW), P())
    return jax.shard_map(local, mesh=torus, in_specs=in_specs, out_specs=out_specs, check_vma=False)
```

time: 208 us -> 193 us (0.928)
  blocking collectives: 186 us -> 176 us
  local copies, waits for them, and re-layouts: 5.12 us -> 0.04 us
  other arithmetic: 2.08 us -> 0 us
    all_to_all x13, blocking collectives: 186 us -> 176 us  [exchange(): return lax.all_to_all(wide, axes, 0, 0, tiled=True).reshape(a.shape)]
    unnamed x24 -> x16, local copies, waits for them, and re-layouts: 4.9 us -> 0.04 us
where the time goes in v2:
time: 193 us; the launch traced here: 192 us
  blocking collectives  176 us (91%)
  Pallas kernels  15.5 us (8%)
    all_to_all x13, blocking collectives, exchange(): return lax.all_to_all(wide, axes, 0, 0, tiled=True).reshape(a.shape)  176 us
    pallas_call x14, Pallas kernels, call(): pl.pallas_call(body, name=name, out_shape=[jax.ShapeDtypeStruct(s, f32) f...  15.5 us

profile of v2, /device:TPU:2, one launch (start us, length us, event | category | flops | bytes accessed | tf_op | source)
XLA Modules:
  0.0 192.5 jit_solution(12648018199741915899)
XLA Ops:
  0.6 0.0 copy-start.3
  0.6 0.0 copy-start.4
  0.7 0.0 copy-start.5
  0.7 2.9 %first_products.1 = (f32[256,128]{1,0:T(8,128)S(1)}, f32[2,8,128]{2,1,0:T(8,128)S(1)}, f32[4,2,256,256]{3,2,1,0:T(8,128)S(1)}, f32[4,2,256,256]{3,2,1,0:T(8,128)S(1)}) custom-call(s32[1,2]{1,0:T(1,128)} %offsets.15, s32[2,4]{1,0:T(2,128)} %bitcast.88, f32[4,2,256,256]{3,2,1,0:T(8,128)} %A_in.1, f32[4,2,256,256]{3,2,1,0:T(8,128)} %G_in.1, f32[128,128]{1,0:T(8,128)} %bitcast.52), custom_call_target="tpu_custom_call" | custom-call | tf_op jit(solution)/shard_map/first_products/pallas_call | solution.py:27
  3.6 15.7 %all_to_all.65 = f32[16,1,2048]{2,1,0:T(1,128)S(1)} all-to-all(f32[16,1,2048]{2,1,0:T(1,128)S(1)} %bitcast.72), channel_id=1, replica_groups=mesh['row_0'=2,'row_1'=4,'row_2'=2,'col_0'=4,'col_1'=4] {'col_0','col_1'}, dimensions={0} | all-to-all | bytes 262144 | tf_op jit(solution)/shard_map/all_to_all | solution.py:331
  19.4 0.0 copy-done.3
  19.4 0.0 copy-done.4
  19.4 0.0 copy-done.5
  19.4 0.0 copy-start
  19.4 0.0 copy-start.1
  19.4 0.0 copy-start.2
  19.4 0.9 first_start.1
  20.3 18.9 %all_to_all.66 = f32[16,1,2048]{2,1,0:T(1,128)S(1)} all-to-all(f32[16,1,2048]{2,1,0:T(1,128)S(1)} %bitcast.73), channel_id=1, replica_groups=mesh['row_0'=2,'row_1'=4,'row_2'=2,'col_0'=4,'col_1'=4] {'row_0','row_1'..., dimensions={0} | all-to-all | bytes 262144 | tf_op jit(solution)/shard_map/all_to_all | solution.py:331
  39.2 0.0 copy-done
  39.2 0.0 copy-done.1
  39.2 0.0 copy-done.2
  39.2 1.0 begin_solve_0.1
  40.2 12.1 %all_to_all.67 = f32[16,1,2176]{2,1,0:T(1,128)S(1)} all-to-all(f32[16,1,2176]{2,1,0:T(1,128)S(1)} %bitcast.71), channel_id=1, replica_groups=mesh['row_0'=2,'row_1'=4,'row_2'=2,'col_0'=4,'col_1'=4] {'col_0','col_1'}, dimensions={0} | all-to-all | bytes 278528 | tf_op jit(solution)/shard_map/all_to_all | solution.py:331
  52.3 0.9 first_image.2
  53.3 13.3 %all_to_all.68 = f32[16,1,2176]{2,1,0:T(1,128)S(1)} all-to-all(f32[16,1,2176]{2,1,0:T(1,128)S(1)} %bitcast.66), channel_id=1, replica_groups=mesh['row_0'=2,'row_1'=4,'row_2'=2,'col_0'=4,'col_1'=4] {'row_0','row_1'..., dimensions={0} | all-to-all | bytes 278528 | tf_op jit(solution)/shard_map/all_to_all | solution.py:331
  66.6 0.0 copy-start.6
  66.6 0.0 copy-start.7
  66.6 1.1 first_step.2
  67.7 12.2 %all_to_all.69 = f32[16,1,2176]{2,1,0:T(1,128)S(1)} all-to-all(f32[16,1,2176]{2,1,0:T(1,128)S(1)} %bitcast.68), channel_id=1, replica_groups=mesh['row_0'=2,'row_1'=4,'row_2'=2,'col_0'=4,'col_1'=4] {'col_0','col_1'}, dimensions={0} | all-to-all | bytes 278528 | tf_op jit(solution)/shard_map/all_to_all | solution.py:331
  79.9 0.8 second_images.2
  80.7 12.5 %all_to_all.70 = f32[16,1,128]{2,1,0:T(1,128)S(1)} all-to-all(f32[16,1,128]{2,1,0:T(1,128)S(1)} %bitcast.86), channel_id=1, replica_groups=mesh['row_0'=2,'row_1'=4,'row_2'=2,'col_0'=4,'col_1'=4] {'row_0','row_1'..., dimensions={0} | all-to-all | bytes 16384 | tf_op jit(solution)/shard_map/all_to_all | solution.py:331
  93.2 0.0 copy-done.6
  93.2 0.0 copy-done.7
  93.2 1.5 update_0.1
  94.7 14.7 %all_to_all.71 = f32[16,1,4096]{2,1,0:T(1,128)S(1)} all-to-all(f32[16,1,4096]{2,1,0:T(1,128)S(1)} %bitcast.64), channel_id=1, replica_groups=mesh['row_0'=2,'row_1'=4,'row_2'=2,'col_0'=4,'col_1'=4] {'row_0','row_1'..., dimensions={0} | all-to-all | bytes 524288 | tf_op jit(solution)/shard_map/all_to_all | solution.py:331
  109.4 1.0 begin_solve_1.1
  110.4 13.7 %all_to_all.72 = f32[16,1,2176]{2,1,0:T(1,128)S(1)} all-to-all(f32[16,1,2176]{2,1,0:T(1,128)S(1)} %bitcast.69), channel_id=1, replica_groups=mesh['row_0'=2,'row_1'=4,'row_2'=2,'col_0'=4,'col_1'=4] {'col_0','col_1'}, dimensions={0} | all-to-all | bytes 278528 | tf_op jit(solution)/shard_map/all_to_all | solution.py:331
  124.1 0.9 first_image.3
  125.1 13.3 %all_to_all.73 = f32[16,1,2176]{2,1,0:T(1,128)S(1)} all-to-all(f32[16,1,2176]{2,1,0:T(1,128)S(1)} %bitcast.67), channel_id=1, replica_groups=mesh['row_0'=2,'row_1'=4,'row_2'=2,'col_0'=4,'col_1'=4] {'row_0','row_1'..., dimensions={0} | all-to-all | bytes 278528 | tf_op jit(solution)/shard_map/all_to_all | solution.py:331
  138.4 1.1 first_step.3
  139.5 12.2 %all_to_all.74 = f32[16,1,2176]{2,1,0:T(1,128)S(1)} all-to-all(f32[16,1,2176]{2,1,0:T(1,128)S(1)} %bitcast.70), channel_id=1, replica_groups=mesh['row_0'=2,'row_1'=4,'row_2'=2,'col_0'=4,'col_1'=4] {'col_0','col_1'}, dimensions={0} | all-to-all | bytes 278528 | tf_op jit(solution)/shard_map/all_to_all | solution.py:331
  151.7 0.8 second_images.3
  152.5 12.5 %all_to_all.75 = f32[16,1,128]{2,1,0:T(1,128)S(1)} all-to-all(f32[16,1,128]{2,1,0:T(1,128)S(1)} %bitcast.87), channel_id=1, replica_groups=mesh['row_0'=2,'row_1'=4,'row_2'=2,'col_0'=4,'col_1'=4] {'row_0','row_1'..., dimensions={0} | all-to-all | bytes 16384 | tf_op jit(solution)/shard_map/all_to_all | solution.py:331
  165.0 1.2 update_1.1
  166.2 13.3 %all_to_all.76 = f32[16,1,2176]{2,1,0:T(1,128)S(1)} all-to-all(f32[16,1,2176]{2,1,0:T(1,128)S(1)} %bitcast.65), channel_id=1, replica_groups=mesh['row_0'=2,'row_1'=4,'row_2'=2,'col_0'=4,'col_1'=4] {'row_0','row_1'..., dimensions={0} | all-to-all | bytes 278528 | tf_op jit(solution)/shard_map/all_to_all | solution.py:331
  179.5 0.6 last_dual.1
  180.1 11.7 %all_to_all.77 = f32[16,1,128]{2,1,0:T(1,128)S(1)} all-to-all(f32[16,1,128]{2,1,0:T(1,128)S(1)} %bitcast.76), channel_id=1, replica_groups=mesh['row_0'=2,'row_1'=4,'row_2'=2,'col_0'=4,'col_1'=4] {'col_0','col_1'}, dimensions={0} | all-to-all | bytes 16384 | tf_op jit(solution)/shard_map/all_to_all | solution.py:331
  191.9 0.6 finish.1
Async XLA Ops:
  0.6 18.7 %copy-start.3 = (s32[1,2]{1,0:T(1,128)S(1)}, s32[1,2]{1,0:T(1,128)}, u32[]{:S(2)}) copy-start(s32[1,2]{1,0:T(1,128)} %offsets.15) | copy-start | bytes 28
  0.6 18.7 %copy-start.4 = (f32[1024]{0:T(1024)S(1)}, f32[1024]{0:T(1024)}, u32[]{:S(2)}) copy-start(f32[1024]{0:T(1024)} %param.20) | copy-start | bytes 12292
  0.7 18.7 %copy-start.5 = (f32[1024]{0:T(1024)S(1)}, f32[1024]{0:T(1024)}, u32[]{:S(2)}) copy-start(f32[1024]{0:T(1024)} %param.21) | copy-start | bytes 12292
  19.4 19.9 %copy-start = (f32[16384]{0:T(1024)S(1)}, f32[16384]{0:T(1024)}, u32[]{:S(2)}) copy-start(f32[16384]{0:T(1024)} %param.16) | copy-start | bytes 196612
  19.4 19.8 %copy-start.1 = (f32[16384]{0:T(1024)S(1)}, f32[16384]{0:T(1024)}, u32[]{:S(2)}) copy-start(f32[16384]{0:T(1024)} %param.15) | copy-start | bytes 196612
  19.4 19.8 %copy-start.2 = (f32[16384]{0:T(1024)S(1)}, f32[16384]{0:T(1024)}, u32[]{:S(2)}) copy-start(f32[16384]{0:T(1024)} %param.19) | copy-start | bytes 196612
  66.6 26.7 %copy-start.6 = (f32[1024]{0:T(1024)S(1)}, f32[1024]{0:T(1024)}, u32[]{:S(2)}) copy-start(f32[1024]{0:T(1024)} %param.17) | copy-start | bytes 12292
  66.6 26.7 %copy-start.7 = (f32[1024]{0:T(1024)S(1)}, f32[1024]{0:T(1024)}, u32[]{:S(2)}) copy-start(f32[1024]{0:T(1024)} %param.18) | copy-start | bytes 12292

commit v3 on v2

--- a/solution.py
+++ b/solution.py
@@ -19,7 +19,6 @@
 
 f32 = jnp.float32
 VMEM = pl.BlockSpec(memory_space=pltpu.VMEM)
-SMEM = pl.BlockSpec(memory_space=pltpu.SMEM)
 
 
 def kernel_call(body, name, outs, scratch=(), spaces=None):
@@ -28,7 +27,7 @@
             body,
             name=name,
             out_shape=[jax.ShapeDtypeStruct(s, f32) for s in outs],
-            in_specs=spaces or [SMEM] + [VMEM] * (len(arrays) - 1),
+            in_specs=spaces or [VMEM] * len(arrays),
             out_specs=[VMEM] * len(outs),
             scratch_shapes=[pltpu.VMEM(s, f32) if isinstance(s, tuple) else s for s in scratch],
             compiler_params=pltpu.CompilerParams(vmem_limit_bytes=8 << 20),
@@ -175,7 +174,7 @@
     return rho_step * z - y - rho_step * ax, -gx
 
 
-def first_start(offsets, A, G, pat, recv, z, y, out, gx_out, ax_out, line):
+def first_start(A, G, pat, recv, z, y, out, gx_out, ax_out, line):
     gx = peer_total(recv, 16, 0, 8)
     ax = peer_total(recv, 16, 8, 16)
     gx_out[...] = gx
@@ -204,7 +203,7 @@
         dual_out[...] = jnp.max(jnp.abs(residual), axis=0, keepdims=True)
 
 
-def first_image(offsets, A, G, pat, recv, out, gd_out, ad_out, sc_out, line):
+def first_image(A, G, pat, recv, out, gd_out, ad_out, sc_out, line):
     gd = peer_total(recv, 17, 0, 8)
     ad = peer_total(recv, 17, 8, 16)
     gd_out[...] = gd
@@ -235,7 +234,7 @@
     to_all(line, out)
 
 
-def second_images(offsets, recv, gd, ad, sc, out, gd_out, ad_out, small_out):
+def second_images(recv, gd, ad, sc, out, gd_out, ad_out, small_out):
     now = peer_total(recv, 17, 16, 17)
     norm, weighted_rem, weighted_mix = now[:, 0:1], now[:, 1:2], now[:, 2:3]
     norm_old, weighted_old = sc[0:1, 0:1], sc[0:1, 1:2]
@@ -251,7 +250,7 @@
 
 
 def update(
-    offsets, A, G, pat, recv, small, step, gd, ad, gd2, ad2, gx, ax, x, rem, d, z, y, lo, hi,
+    A, G, pat, recv, small, step, gd, ad, gd2, ad2, gx, ax, x, rem, d, z, y, lo, hi,
     *rest, last,
 ):
     if last:
@@ -350,7 +349,7 @@
     )(*[pltpu.with_memory_space_constraint(a, pltpu.HBM) for a in (offsets, block_pattern.T, A, G, x)])
     recv = exchange(out, COL)
     out, gx, ax = kernel_call(first_start, "first_start", [payload(16), R8, R8], [(16, LANES)])(
-        offsets, A, G, pat, recv, z, y
+        A, G, pat, recv, z, y
     )
     primal0 = dual0 = None
     for outer in range(2):
@@ -369,17 +368,17 @@
         recv = exchange(out, COL)
         out, gd, ad, sc = kernel_call(
             first_image, "first_image", [payload(17), R8, R8, ONE], [(24, LANES)]
-        )(offsets, A, G, pat, recv)
+        )(A, G, pat, recv)
         recv = exchange(out, ROW)
         out, rem, step = kernel_call(
             first_step, "first_step", [payload(17), V, ONE], [(24, LANES), RING, TURN]
         )(offsets, A, G, pat, recv, d, sc, diag)
         recv = exchange(out, COL)
         out, gd2, ad2, small = kernel_call(second_images, "second_images", [payload(1), R8, R8, ONE])(
-            offsets, recv, gd, ad, sc
+            recv, gd, ad, sc
         )
         recv = exchange(out, ROW)
-        args = (offsets, A, G, pat, recv, small, step, gd, ad, gd2, ad2, gx, ax, x, rem, d, z, y, lo, hi)
+        args = (A, G, pat, recv, small, step, gd, ad, gd2, ad2, gx, ax, x, rem, d, z, y, lo, hi)
         if outer == 0:
 
             def body(*refs):
@@ -399,7 +398,7 @@
     recv = exchange(out, ROW)
     (out,) = kernel_call(last_dual, "last_dual", [payload(1)], [TURN])(offsets, recv, base, dual0)
     recv = exchange(out, COL)
-    x, z, y, residuals = kernel_call(finish, "finish", [V, R8, R8, (2, 2)], (), [VMEM] * 4)(recv, x, z, y)
+    x, z, y, residuals = kernel_call(finish, "finish", [V, R8, R8, (2, 2)])(recv, x, z, y)
     return x.reshape(-1), z.reshape(-1), y.reshape(-1), residuals
 
 

time: 193 us -> 187 us (0.969)
  Pallas kernels: 15.5 us -> 9.26 us
    pallas_call x14, Pallas kernels: 15.5 us -> 9.26 us  [call(): pl.pallas_call(body, name=name, out_shape=[jax.ShapeDtypeStruct(s, f32) f...]
where the time goes in v3:
time: 187 us; the launch traced here: 186 us
  blocking collectives  176 us (94%)
  Pallas kernels  9.26 us (5%)
    all_to_all x13, blocking collectives, exchange(): return lax.all_to_all(wide, axes, 0, 0, tiled=True).reshape(a.shape)  176 us
    pallas_call x14, Pallas kernels, call(): pl.pallas_call(body, name=name, out_shape=[jax.ShapeDtypeStruct(s, f32) f...  9.26 us

profile of v3, /device:TPU:2, one launch (start us, length us, event | category | flops | bytes accessed | tf_op | source)
XLA Modules:
  0.0 186.2 jit_solution(14174894425850306976)
XLA Ops:
  0.6 0.0 copy-start.4
  0.6 0.0 copy-start.5
  0.7 2.9 %first_products.1 = (f32[256,128]{1,0:T(8,128)S(1)}, f32[2,8,128]{2,1,0:T(8,128)S(1)}, f32[4,2,256,256]{3,2,1,0:T(8,128)S(1)}, f32[4,2,256,256]{3,2,1,0:T(8,128)S(1)}) custom-call(s32[1,2]{1,0:T(1,128)} %offsets.5, s32[2,4]{1,0:T(2,128)} %bitcast.88, f32[4,2,256,256]{3,2,1,0:T(8,128)} %A_in.1, f32[4,2,256,256]{3,2,1,0:T(8,128)} %G_in.1, f32[128,128]{1,0:T(8,128)} %bitcast.49), custom_call_target="tpu_custom_call" | custom-call | tf_op jit(solution)/shard_map/first_products/pallas_call | solution.py:26
  3.6 15.7 %all_to_all.65 = f32[16,1,2048]{2,1,0:T(1,128)S(1)} all-to-all(f32[16,1,2048]{2,1,0:T(1,128)S(1)} %bitcast.72), channel_id=1, replica_groups=mesh['row_0'=2,'row_1'=4,'row_2'=2,'col_0'=4,'col_1'=4] {'col_0','col_1'}, dimensions={0} | all-to-all | bytes 262144 | tf_op jit(solution)/shard_map/all_to_all | solution.py:330
  19.3 0.0 copy-done.4
  19.4 0.0 copy-done.5
  19.4 0.0 copy-start
  19.4 0.0 copy-start.1
  19.4 0.0 copy-start.2
  19.4 0.0 copy-start.3
  19.4 0.4 first_start.1
  19.8 18.9 %all_to_all.66 = f32[16,1,2048]{2,1,0:T(1,128)S(1)} all-to-all(f32[16,1,2048]{2,1,0:T(1,128)S(1)} %bitcast.73), channel_id=1, replica_groups=mesh['row_0'=2,'row_1'=4,'row_2'=2,'col_0'=4,'col_1'=4] {'row_0','row_1'..., dimensions={0} | all-to-all | bytes 262144 | tf_op jit(solution)/shard_map/all_to_all | solution.py:330
  38.7 0.0 copy-done
  38.7 0.0 copy-done.1
  38.7 0.0 copy-done.2
  38.7 0.0 copy-done.3
  38.7 0.5 begin_solve_0.1
  39.2 12.1 %all_to_all.67 = f32[16,1,2176]{2,1,0:T(1,128)S(1)} all-to-all(f32[16,1,2176]{2,1,0:T(1,128)S(1)} %bitcast.71), channel_id=1, replica_groups=mesh['row_0'=2,'row_1'=4,'row_2'=2,'col_0'=4,'col_1'=4] {'col_0','col_1'}, dimensions={0} | all-to-all | bytes 278528 | tf_op jit(solution)/shard_map/all_to_all | solution.py:330
  51.3 0.4 first_image.2
  51.7 13.3 %all_to_all.68 = f32[16,1,2176]{2,1,0:T(1,128)S(1)} all-to-all(f32[16,1,2176]{2,1,0:T(1,128)S(1)} %bitcast.66), channel_id=1, replica_groups=mesh['row_0'=2,'row_1'=4,'row_2'=2,'col_0'=4,'col_1'=4] {'row_0','row_1'..., dimensions={0} | all-to-all | bytes 278528 | tf_op jit(solution)/shard_map/all_to_all | solution.py:330
  65.0 0.0 copy-start.6
  65.0 0.0 copy-start.7
  65.0 0.6 first_step.2
  65.6 12.2 %all_to_all.69 = f32[16,1,2176]{2,1,0:T(1,128)S(1)} all-to-all(f32[16,1,2176]{2,1,0:T(1,128)S(1)} %bitcast.68), channel_id=1, replica_groups=mesh['row_0'=2,'row_1'=4,'row_2'=2,'col_0'=4,'col_1'=4] {'col_0','col_1'}, dimensions={0} | all-to-all | bytes 278528 | tf_op jit(solution)/shard_map/all_to_all | solution.py:330
  77.8 0.2 second_images.2
  78.0 12.5 %all_to_all.70 = f32[16,1,128]{2,1,0:T(1,128)S(1)} all-to-all(f32[16,1,128]{2,1,0:T(1,128)S(1)} %bitcast.86), channel_id=1, replica_groups=mesh['row_0'=2,'row_1'=4,'row_2'=2,'col_0'=4,'col_1'=4] {'row_0','row_1'..., dimensions={0} | all-to-all | bytes 16384 | tf_op jit(solution)/shard_map/all_to_all | solution.py:330
  90.6 0.0 copy-done.6
  90.6 0.0 copy-done.7
  90.6 1.0 update_0.1
  91.5 14.7 %all_to_all.71 = f32[16,1,4096]{2,1,0:T(1,128)S(1)} all-to-all(f32[16,1,4096]{2,1,0:T(1,128)S(1)} %bitcast.64), channel_id=1, replica_groups=mesh['row_0'=2,'row_1'=4,'row_2'=2,'col_0'=4,'col_1'=4] {'row_0','row_1'..., dimensions={0} | all-to-all | bytes 524288 | tf_op jit(solution)/shard_map/all_to_all | solution.py:330
  106.2 0.6 begin_solve_1.1
  106.8 13.7 %all_to_all.72 = f32[16,1,2176]{2,1,0:T(1,128)S(1)} all-to-all(f32[16,1,2176]{2,1,0:T(1,128)S(1)} %bitcast.69), channel_id=1, replica_groups=mesh['row_0'=2,'row_1'=4,'row_2'=2,'col_0'=4,'col_1'=4] {'col_0','col_1'}, dimensions={0} | all-to-all | bytes 278528 | tf_op jit(solution)/shard_map/all_to_all | solution.py:330
  120.5 0.4 first_image.3
  120.9 13.3 %all_to_all.73 = f32[16,1,2176]{2,1,0:T(1,128)S(1)} all-to-all(f32[16,1,2176]{2,1,0:T(1,128)S(1)} %bitcast.67), channel_id=1, replica_groups=mesh['row_0'=2,'row_1'=4,'row_2'=2,'col_0'=4,'col_1'=4] {'row_0','row_1'..., dimensions={0} | all-to-all | bytes 278528 | tf_op jit(solution)/shard_map/all_to_all | solution.py:330
  134.2 0.6 first_step.3
  134.8 12.2 %all_to_all.74 = f32[16,1,2176]{2,1,0:T(1,128)S(1)} all-to-all(f32[16,1,2176]{2,1,0:T(1,128)S(1)} %bitcast.70), channel_id=1, replica_groups=mesh['row_0'=2,'row_1'=4,'row_2'=2,'col_0'=4,'col_1'=4] {'col_0','col_1'}, dimensions={0} | all-to-all | bytes 278528 | tf_op jit(solution)/shard_map/all_to_all | solution.py:330
  147.0 0.2 second_images.3
  147.2 12.5 %all_to_all.75 = f32[16,1,128]{2,1,0:T(1,128)S(1)} all-to-all(f32[16,1,128]{2,1,0:T(1,128)S(1)} %bitcast.87), channel_id=1, replica_groups=mesh['row_0'=2,'row_1'=4,'row_2'=2,'col_0'=4,'col_1'=4] {'row_0','row_1'..., dimensions={0} | all-to-all | bytes 16384 | tf_op jit(solution)/shard_map/all_to_all | solution.py:330
  159.8 0.6 update_1.1
  160.4 13.3 %all_to_all.76 = f32[16,1,2176]{2,1,0:T(1,128)S(1)} all-to-all(f32[16,1,2176]{2,1,0:T(1,128)S(1)} %bitcast.65), channel_id=1, replica_groups=mesh['row_0'=2,'row_1'=4,'row_2'=2,'col_0'=4,'col_1'=4] {'row_0','row_1'..., dimensions={0} | all-to-all | bytes 278528 | tf_op jit(solution)/shard_map/all_to_all | solution.py:330
  173.7 0.2 last_dual.1
  173.9 11.7 %all_to_all.77 = f32[16,1,128]{2,1,0:T(1,128)S(1)} all-to-all(f32[16,1,128]{2,1,0:T(1,128)S(1)} %bitcast.77), channel_id=1, replica_groups=mesh['row_0'=2,'row_1'=4,'row_2'=2,'col_0'=4,'col_1'=4] {'col_0','col_1'}, dimensions={0} | all-to-all | bytes 16384 | tf_op jit(solution)/shard_map/all_to_all | solution.py:330
  185.6 0.6 finish.1
Async XLA Ops:
  0.6 18.7 %copy-start.4 = (f32[1024]{0:T(1024)S(1)}, f32[1024]{0:T(1024)}, u32[]{:S(2)}) copy-start(f32[1024]{0:T(1024)} %param.20) | copy-start | bytes 12292
  0.6 18.7 %copy-start.5 = (f32[1024]{0:T(1024)S(1)}, f32[1024]{0:T(1024)}, u32[]{:S(2)}) copy-start(f32[1024]{0:T(1024)} %param.21) | copy-start | bytes 12292
  19.4 19.3 %copy-start = (f32[16384]{0:T(1024)S(1)}, f32[16384]{0:T(1024)}, u32[]{:S(2)}) copy-start(f32[16384]{0:T(1024)} %param.16) | copy-start | bytes 196612
  19.4 19.3 %copy-start.1 = (f32[16384]{0:T(1024)S(1)}, f32[16384]{0:T(1024)}, u32[]{:S(2)}) copy-start(f32[16384]{0:T(1024)} %param.19) | copy-start | bytes 196612
  19.4 19.3 %copy-start.2 = (f32[16384]{0:T(1024)S(1)}, f32[16384]{0:T(1024)}, u32[]{:S(2)}) copy-start(f32[16384]{0:T(1024)} %param.15) | copy-start | bytes 196612
  19.4 19.3 %copy-start.3 = (s32[1,2]{1,0:T(1,128)S(1)}, s32[1,2]{1,0:T(1,128)}, u32[]{:S(2)}) copy-start(s32[1,2]{1,0:T(1,128)} %offsets.5) | copy-start | bytes 28
  65.0 25.6 %copy-start.6 = (f32[1024]{0:T(1024)S(1)}, f32[1024]{0:T(1024)}, u32[]{:S(2)}) copy-start(f32[1024]{0:T(1024)} %param.17) | copy-start | bytes 12292
  65.0 25.6 %copy-start.7 = (f32[1024]{0:T(1024)S(1)}, f32[1024]{0:T(1024)}, u32[]{:S(2)}) copy-start(f32[1024]{0:T(1024)} %param.18) | copy-start | bytes 12292

commit v4 on v3

--- a/solution.py
+++ b/solution.py
@@ -184,12 +184,12 @@
     to_all(line, out)
 
 
-def begin_solve(offsets, A, G, pat, recv, x, diag, lin, out, rem_out, *rest, dual):
+def begin_solve(offsets, A, G, pat, recv, x, diag, lin, *rest, dual):
     if dual:
-        dual_out, line, ring, turn = rest
+        own, out, rem_out, dual_out, line, ring, turn = rest
     else:
-        line, ring, turn = rest
-    each = 32 if dual else 16
+        out, rem_out, line, ring, turn = rest
+    each = 24 if dual else 16
     start = assemble(offsets, recv, each, 0, turn)
     xv = x[...]
     shifted = diag[...] + sigma_shift
@@ -199,8 +199,26 @@
     line[16:17, :] = packed((full_total(rem * rem), full_total(rem * shifted * rem)))
     to_all(line, out)
     if dual:
-        residual = diag[...] * xv + lin[...] + assemble(offsets, recv, each, 16, turn)
-        dual_out[...] = jnp.max(jnp.abs(residual), axis=0, keepdims=True)
+        base = diag[...] * xv + lin[...]
+        ring[0:VROWS, :] = base
+        ring[VROWS : VROWS + 8, :] = base[0:8, :]
+        mine = ring[pl.ds(first_touched(offsets, 0), 8), :]
+        dual_out[...] = jnp.abs(mine + own[...] + peer_total(recv, 24, 16, 24))
+
+
+def to_owners(offsets, line, spread, out):
+    shift = (offsets[0, 1] - offsets[0, 0]) % 64
+    spread[0:8, :] = jnp.zeros((8, LANES), f32)
+    spread[8:16, :] = line[24:32, :]
+    spread[16:24, :] = jnp.zeros((8, LANES), f32)
+    inner = 2 * (shift % 4)
+    near = spread[pl.ds(8 - inner, 8), :]
+    far = spread[pl.ds(16 - inner, 8), :]
+    owner = (lax.axis_index(ROW) + shift // 4) % PEERS
+    for peer in range(PEERS):
+        here = jnp.where(owner == peer, 1.0, 0.0)
+        after = jnp.where((owner + 1) % PEERS == peer, 1.0, 0.0)
+        out[24 * peer + 16 : 24 * peer + 24, :] = here * near + after * far
 
 
 def first_image(A, G, pat, recv, out, gd_out, ad_out, sc_out, line):
@@ -250,13 +268,12 @@
 
 
 def update(
-    A, G, pat, recv, small, step, gd, ad, gd2, ad2, gx, ax, x, rem, d, z, y, lo, hi,
-    *rest, last,
+    A, G, pat, recv, small, step, gd, ad, gd2, ad2, gx, ax, x, rem, d, z, y, lo, hi, *rest, last,
 ):
     if last:
-        diag, lin, primal0, out, x_out, z_out, y_out, base_out, line = rest
+        diag, lin, primal0, dual0, out, x_out, z_out, y_out, base_out, line = rest
     else:
-        out, x_out, z_out, y_out, gx_out, ax_out, primal_out, line = rest
+        offsets, out, x_out, z_out, y_out, gx_out, ax_out, primal_out, own_out, line, spread = rest
     squares = full_total(recv[...])
     norm, weighted, ratio = small[0:1, 0:1], small[0:1, 1:2], small[0:1, 2:3]
     step2 = norm / (squares + weighted)
@@ -275,15 +292,23 @@
     primal = full_max(jnp.abs(ax_new - z_new))
     if last:
         backward(((G, gx_new), (A, y_new)), pat, line, 0)
-        line[16:17, :] = packed((primal0[0:1, 0:1], primal))
+        line[16:17, :] = packed((primal0[0:1, 0:1], primal, full_max(dual0[...])))
+        to_all(line, out)
     else:
         gx_out[...] = gx_new
         ax_out[...] = ax_new
         primal_out[...] = jnp.broadcast_to(primal, (1, LANES))
-        va, vg = start_rows(z_new, y_new, gx_new, ax_new)
-        backward(((A, va), (G, vg)), pat, line, 0)
-        backward(((G, gx_new), (A, y_new)), pat, line, 16)
-    to_all(line, out)
+        va, _ = start_rows(z_new, y_new, gx_new, ax_new)
+        backward(((G, gx_new),), pat, line, 32)
+        backward(((A, va),), pat, line, 0)
+        backward(((A, y_new),), pat, line, 16)
+        both = line[32:48, :]
+        line[16:32, :] = line[16:32, :] + both
+        own_out[...] = line[16:24, :]
+        start = line[0:16, :] - both
+        for peer in range(PEERS):
+            out[24 * peer : 24 * peer + 16, :] = start
+        to_owners(offsets, line, spread, out)
     dv = d[...]
     xv = x[...]
     solved = xv + step1 * dv + step2 * (rem[...] + ratio * dv)
@@ -293,14 +318,12 @@
         base_out[...] = diag[...] * x_new + lin[...]
 
 
-def last_dual(offsets, recv, base, dual0, out, turn):
+def last_dual(offsets, recv, base, out, turn):
     residual = base[...] + assemble(offsets, recv, 17, 0, turn)
-    primal = recv[16:17, :]
+    top = recv[16:17, :]
     for peer in range(1, PEERS):
-        primal = jnp.maximum(primal, recv[17 * peer + 16 : 17 * peer + 17, :])
-    row = packed(
-        (primal[:, 0:1], primal[:, 1:2], full_max(dual0[...]), full_max(jnp.abs(residual)))
-    )
+        top = jnp.maximum(top, recv[17 * peer + 16 : 17 * peer + 17, :])
+    row = packed((top[:, 0:1], top[:, 1:2], top[:, 2:3], full_max(jnp.abs(residual))))
     out[...] = jnp.broadcast_to(row, (PEERS, LANES))
 
 
@@ -328,6 +351,20 @@
 def exchange(a, axes):
     wide = a.reshape(PEERS, 1, -1)
     return lax.all_to_all(wide, axes, 0, 0, tiled=True).reshape(a.shape)
+
+
+def near_rows():
+    groups = []
+    for col in range(16):
+        near, far = list(range(0, 8)), list(range(8, 16))
+        groups.append([16 * row + col for row in near] + [16 * row + (col ^ 2) for row in far])
+    return groups
+
+
+def exchange_near(a):
+    wide = a.reshape(PEERS, 1, -1)
+    got = lax.all_to_all(wide, ROW + COL, 0, 0, axis_index_groups=near_rows(), tiled=True)
+    return got.reshape(a.shape)
 
 
 def local(
@@ -354,13 +391,13 @@
     primal0 = dual0 = None
     for outer in range(2):
         recv = exchange(out, ROW)
-        shapes = [payload(17), V] + ([ONE] if outer else [])
+        shapes = [payload(17), V] + ([R8] if outer else [])
 
         def body(*refs, dual=bool(outer)):
             begin_solve(*refs, dual=dual)
 
         got = kernel_call(body, f"begin_solve_{outer}", shapes, [(24, LANES), RING, TURN])(
-            offsets, A, G, pat, recv, x, diag, lin
+            offsets, A, G, pat, recv, x, diag, lin, *([own] if outer else [])
         )
         out, d = got[:2]
         if outer:
@@ -377,16 +414,17 @@
         out, gd2, ad2, small = kernel_call(second_images, "second_images", [payload(1), R8, R8, ONE])(
             recv, gd, ad, sc
         )
-        recv = exchange(out, ROW)
+        recv = exchange_near(out)
         args = (A, G, pat, recv, small, step, gd, ad, gd2, ad2, gx, ax, x, rem, d, z, y, lo, hi)
         if outer == 0:
 
             def body(*refs):
                 update(*refs, last=False)
 
-            out, x, z, y, gx, ax, primal0 = kernel_call(
-                body, "update_0", [payload(32), V, R8, R8, R8, R8, ONE], [(32, LANES)]
-            )(*args)
+            out, x, z, y, gx, ax, primal0, own = kernel_call(
+                body, "update_0", [payload(24), V, R8, R8, R8, R8, ONE, R8],
+                [(48, LANES), (24, LANES)],
+            )(*args, offsets)
         else:
 
             def body(*refs):
@@ -394,9 +432,9 @@
 
             out, x, z, y, base = kernel_call(
                 body, "update_1", [payload(17), V, R8, R8, V], [(24, LANES)]
-            )(*args, diag, lin, primal0)
+            )(*args, diag, lin, primal0, dual0)
     recv = exchange(out, ROW)
-    (out,) = kernel_call(last_dual, "last_dual", [payload(1)], [TURN])(offsets, recv, base, dual0)
+    (out,) = kernel_call(last_dual, "last_dual", [payload(1)], [TURN])(offsets, recv, base)
     recv = exchange(out, COL)
     x, z, y, residuals = kernel_call(finish, "finish", [V, R8, R8, (2, 2)])(recv, x, z, y)
     return x.reshape(-1), z.reshape(-1), y.reshape(-1), residuals

time: 187 us -> 185 us (0.989)
  blocking collectives: 176 us -> 174 us
    all_to_all x13 -> x11, blocking collectives: 176 us -> 153 us  [exchange(): return lax.all_to_all(wide, axes, 0, 0, tiled=True).reshape(a.shape)]
    all_to_all x0 -> x2, blocking collectives: none -> 21.5 us  [exchange_near(): lax.all_to_all(wide, ROW + COL, 0, 0, axis_index_groups=near_rows(), tile...]
where the time goes in v4:
time: 185 us; the launch traced here: 184 us
  blocking collectives  174 us (94%)
  Pallas kernels  9.03 us (5%)
    all_to_all x11, blocking collectives, exchange(): return lax.all_to_all(wide, axes, 0, 0, tiled=True).reshape(a.shape)  153 us
    all_to_all x2, blocking collectives, exchange_near(): lax.all_to_all(wide, ROW + COL, 0, 0, axis_index_groups=near_rows(), tile...  21.5 us
    pallas_call x14, Pallas kernels, call(): pl.pallas_call(body, name=name, out_shape=[jax.ShapeDtypeStruct(s, f32) f...  9.03 us

profile of v4, /device:TPU:2, one launch (start us, length us, event | category | flops | bytes accessed | tf_op | source)
XLA Modules:
  0.0 184.3 jit_solution(280404084675241999)
XLA Ops:
  0.6 0.0 copy-start.6
  0.6 0.0 copy-start.7
  0.7 2.9 %first_products.1 = (f32[256,128]{1,0:T(8,128)S(1)}, f32[2,8,128]{2,1,0:T(8,128)S(1)}, f32[4,2,256,256]{3,2,1,0:T(8,128)S(1)}, f32[4,2,256,256]{3,2,1,0:T(8,128)S(1)}) custom-call(s32[1,2]{1,0:T(1,128)} %offsets.5, s32[2,4]{1,0:T(2,128)} %bitcast.88, f32[4,2,256,256]{3,2,1,0:T(8,128)} %A_in.1, f32[4,2,256,256]{3,2,1,0:T(8,128)} %G_in.1, f32[128,128]{1,0:T(8,128)} %bitcast.52), custom_call_target="tpu_custom_call" | custom-call | tf_op jit(solution)/shard_map/first_products/pallas_call | solution.py:26
  3.6 15.7 %all_to_all.65 = f32[16,1,2048]{2,1,0:T(1,128)S(1)} all-to-all(f32[16,1,2048]{2,1,0:T(1,128)S(1)} %bitcast.72), channel_id=1, replica_groups=mesh['row_0'=2,'row_1'=4,'row_2'=2,'col_0'=4,'col_1'=4] {'col_0','col_1'}, dimensions={0} | all-to-all | bytes 262144 | tf_op jit(solution)/shard_map/all_to_all | solution.py:353
  19.3 0.0 copy-done.6
  19.4 0.0 copy-done.7
  19.4 0.0 copy-start
  19.4 0.0 copy-start.1
  19.4 0.0 copy-start.2
  19.4 0.0 copy-start.3
  19.4 0.4 first_start.1
  19.8 18.9 %all_to_all.66 = f32[16,1,2048]{2,1,0:T(1,128)S(1)} all-to-all(f32[16,1,2048]{2,1,0:T(1,128)S(1)} %bitcast.73), channel_id=1, replica_groups=mesh['row_0'=2,'row_1'=4,'row_2'=2,'col_0'=4,'col_1'=4] {'row_0','row_1'..., dimensions={0} | all-to-all | bytes 262144 | tf_op jit(solution)/shard_map/all_to_all | solution.py:353
  38.7 0.0 copy-done
  38.7 0.0 copy-done.1
  38.7 0.0 copy-done.2
  38.7 0.0 copy-done.3
  38.7 0.5 begin_solve_0.1
  39.2 12.1 %all_to_all.67 = f32[16,1,2176]{2,1,0:T(1,128)S(1)} all-to-all(f32[16,1,2176]{2,1,0:T(1,128)S(1)} %bitcast.71), channel_id=1, replica_groups=mesh['row_0'=2,'row_1'=4,'row_2'=2,'col_0'=4,'col_1'=4] {'col_0','col_1'}, dimensions={0} | all-to-all | bytes 278528 | tf_op jit(solution)/shard_map/all_to_all | solution.py:353
  51.3 0.4 first_image.2
  51.7 13.3 %all_to_all.68 = f32[16,1,2176]{2,1,0:T(1,128)S(1)} all-to-all(f32[16,1,2176]{2,1,0:T(1,128)S(1)} %bitcast.66), channel_id=1, replica_groups=mesh['row_0'=2,'row_1'=4,'row_2'=2,'col_0'=4,'col_1'=4] {'row_0','row_1'..., dimensions={0} | all-to-all | bytes 278528 | tf_op jit(solution)/shard_map/all_to_all | solution.py:353
  65.0 0.0 copy-start.4
  65.0 0.0 copy-start.5
  65.0 0.6 first_step.2
  65.6 12.2 %all_to_all.69 = f32[16,1,2176]{2,1,0:T(1,128)S(1)} all-to-all(f32[16,1,2176]{2,1,0:T(1,128)S(1)} %bitcast.69), channel_id=1, replica_groups=mesh['row_0'=2,'row_1'=4,'row_2'=2,'col_0'=4,'col_1'=4] {'col_0','col_1'}, dimensions={0} | all-to-all | bytes 278528 | tf_op jit(solution)/shard_map/all_to_all | solution.py:353
  77.8 0.2 second_images.2
  78.0 10.7 %all_to_all.70 = f32[16,1,128]{2,1,0:T(1,128)S(1)} all-to-all(f32[16,1,128]{2,1,0:T(1,128)S(1)} %bitcast.86), channel_id=1, replica_groups={{0,16,32,48,64,80,96,112,130,146,162,178,194,210,226,242},{1,17,33,49,6..., dimensions={0} | all-to-all | bytes 16384 | tf_op jit(solution)/shard_map/all_to_all | solution.py:366
  88.8 0.0 copy-done.4
  88.8 0.0 copy-done.5
  88.8 0.8 update_0.1
  89.6 14.0 %all_to_all.71 = f32[16,1,3072]{2,1,0:T(1,128)S(1)} all-to-all(f32[16,1,3072]{2,1,0:T(1,128)S(1)} %bitcast.64), channel_id=1, replica_groups=mesh['row_0'=2,'row_1'=4,'row_2'=2,'col_0'=4,'col_1'=4] {'row_0','row_1'..., dimensions={0} | all-to-all | bytes 393216 | tf_op jit(solution)/shard_map/all_to_all | solution.py:353
  103.6 0.5 begin_solve_1.1
  104.1 14.5 %all_to_all.72 = f32[16,1,2176]{2,1,0:T(1,128)S(1)} all-to-all(f32[16,1,2176]{2,1,0:T(1,128)S(1)} %bitcast.67), channel_id=1, replica_groups=mesh['row_0'=2,'row_1'=4,'row_2'=2,'col_0'=4,'col_1'=4] {'col_0','col_1'}, dimensions={0} | all-to-all | bytes 278528 | tf_op jit(solution)/shard_map/all_to_all | solution.py:353
  118.5 0.4 first_image.3
  118.9 13.3 %all_to_all.73 = f32[16,1,2176]{2,1,0:T(1,128)S(1)} all-to-all(f32[16,1,2176]{2,1,0:T(1,128)S(1)} %bitcast.68), channel_id=1, replica_groups=mesh['row_0'=2,'row_1'=4,'row_2'=2,'col_0'=4,'col_1'=4] {'row_0','row_1'..., dimensions={0} | all-to-all | bytes 278528 | tf_op jit(solution)/shard_map/all_to_all | solution.py:353
  132.2 0.6 first_step.3
  132.8 12.2 %all_to_all.74 = f32[16,1,2176]{2,1,0:T(1,128)S(1)} all-to-all(f32[16,1,2176]{2,1,0:T(1,128)S(1)} %bitcast.70), channel_id=1, replica_groups=mesh['row_0'=2,'row_1'=4,'row_2'=2,'col_0'=4,'col_1'=4] {'col_0','col_1'}, dimensions={0} | all-to-all | bytes 278528 | tf_op jit(solution)/shard_map/all_to_all | solution.py:353
  145.0 0.2 second_images.3
  145.3 10.7 %all_to_all.75 = f32[16,1,128]{2,1,0:T(1,128)S(1)} all-to-all(f32[16,1,128]{2,1,0:T(1,128)S(1)} %bitcast.87), channel_id=1, replica_groups={{0,16,32,48,64,80,96,112,130,146,162,178,194,210,226,242},{1,17,33,49,6..., dimensions={0} | all-to-all | bytes 16384 | tf_op jit(solution)/shard_map/all_to_all | solution.py:366
  156.0 0.6 update_1.1
  156.7 13.5 %all_to_all.76 = f32[16,1,2176]{2,1,0:T(1,128)S(1)} all-to-all(f32[16,1,2176]{2,1,0:T(1,128)S(1)} %bitcast.65), channel_id=1, replica_groups=mesh['row_0'=2,'row_1'=4,'row_2'=2,'col_0'=4,'col_1'=4] {'row_0','row_1'..., dimensions={0} | all-to-all | bytes 278528 | tf_op jit(solution)/shard_map/all_to_all | solution.py:353
  170.1 0.2 last_dual.1
  170.3 13.3 %all_to_all.77 = f32[16,1,128]{2,1,0:T(1,128)S(1)} all-to-all(f32[16,1,128]{2,1,0:T(1,128)S(1)} %bitcast.76), channel_id=1, replica_groups=mesh['row_0'=2,'row_1'=4,'row_2'=2,'col_0'=4,'col_1'=4] {'col_0','col_1'}, dimensions={0} | all-to-all | bytes 16384 | tf_op jit(solution)/shard_map/all_to_all | solution.py:353
  183.6 0.6 finish.1
Async XLA Ops:
  0.6 18.7 %copy-start.6 = (f32[1024]{0:T(1024)S(1)}, f32[1024]{0:T(1024)}, u32[]{:S(2)}) copy-start(f32[1024]{0:T(1024)} %param.20) | copy-start | bytes 12292
  0.6 18.7 %copy-start.7 = (f32[1024]{0:T(1024)S(1)}, f32[1024]{0:T(1024)}, u32[]{:S(2)}) copy-start(f32[1024]{0:T(1024)} %param.21) | copy-start | bytes 12292
  19.4 19.3 %copy-start = (f32[16384]{0:T(1024)S(1)}, f32[16384]{0:T(1024)}, u32[]{:S(2)}) copy-start(f32[16384]{0:T(1024)} %param.16) | copy-start | bytes 196612
  19.4 19.3 %copy-start.1 = (f32[16384]{0:T(1024)S(1)}, f32[16384]{0:T(1024)}, u32[]{:S(2)}) copy-start(f32[16384]{0:T(1024)} %param.15) | copy-start | bytes 196612
  19.4 19.3 %copy-start.2 = (f32[16384]{0:T(1024)S(1)}, f32[16384]{0:T(1024)}, u32[]{:S(2)}) copy-start(f32[16384]{0:T(1024)} %param.19) | copy-start | bytes 196612
  19.4 19.3 %copy-start.3 = (s32[1,2]{1,0:T(1,128)S(1)}, s32[1,2]{1,0:T(1,128)}, u32[]{:S(2)}) copy-start(s32[1,2]{1,0:T(1,128)} %offsets.5) | copy-start | bytes 28
  65.0 23.8 %copy-start.4 = (f32[1024]{0:T(1024)S(1)}, f32[1024]{0:T(1024)}, u32[]{:S(2)}) copy-start(f32[1024]{0:T(1024)} %param.17) | copy-start | bytes 12292
  65.0 23.8 %copy-start.5 = (f32[1024]{0:T(1024)S(1)}, f32[1024]{0:T(1024)}, u32[]{:S(2)}) copy-start(f32[1024]{0:T(1024)} %param.18) | copy-start | bytes 12292

commit v5 on v4

--- a/solution.py
+++ b/solution.py
@@ -149,24 +149,23 @@
         pltpu.make_async_copy(offsets_in, offsets, small_sems.at[0]),
         pltpu.make_async_copy(pattern_in, pattern, small_sems.at[1]),
         pltpu.make_async_copy(x_in, ring.at[0:VROWS, :], small_sems.at[2]),
-        pltpu.make_async_copy(x_in.at[0:8, :], ring.at[VROWS : VROWS + 8, :], small_sems.at[3]),
     ]
     big = [
-        [pltpu.make_async_copy(src.at[t], dst.at[t], sems.at[m, t]) for t in range(4)]
+        pltpu.make_async_copy(src, dst, sems.at[m])
         for m, (src, dst) in enumerate(((G_in, G), (A_in, A)))
     ]
-    for copy in small + big[0] + big[1]:
+    for copy in small + big:
         copy.start()
     for copy in small:
         copy.wait()
+    ring[VROWS : VROWS + 8, :] = ring[0:8, :]
     for k in range(2):
         for t in range(4):
             pat_out[k, 2 * t : 2 * t + 2, :] = jnp.full((2, LANES), pattern[k, t].astype(f32))
     touched = [ring[pl.ds(first_touched(offsets, k), 8), :] * pat_out[k] for k in range(2)]
     for m, mat in enumerate((G, A)):
-        for t in range(4):
-            big[m][t].wait()
-            forward_row(mat, t, touched, line, 8 * m)
+        big[m].wait()
+        forward(mat, touched, line, 8 * m)
     to_all(line, out)
 
 
@@ -380,7 +379,7 @@
         first_products, "first_products", [payload(16), (2, 8, LANES), BLOCKS, BLOCKS],
         [
             pltpu.SMEM((1, 2), jnp.int32), pltpu.SMEM((2, 4), jnp.int32), (16, LANES), RING,
-            pltpu.SemaphoreType.DMA((4,)), pltpu.SemaphoreType.DMA((2, 4)),
+            pltpu.SemaphoreType.DMA((3,)), pltpu.SemaphoreType.DMA((2,)),
         ],
         [pl.BlockSpec(memory_space=pltpu.HBM)] * 5,
     )(*[pltpu.with_memory_space_constraint(a, pltpu.HBM) for a in (offsets, block_pattern.T, A, G, x)])

time: 185 us -> 185 us (level)
  no operation moved by 1% of the time
where the time goes in v5:
time: 185 us; the launch traced here: 184 us
  blocking collectives  174 us (94%)
  Pallas kernels  8.61 us (5%)
    all_to_all x11, blocking collectives, exchange(): return lax.all_to_all(wide, axes, 0, 0, tiled=True).reshape(a.shape)  153 us
    all_to_all x2, blocking collectives, exchange_near(): lax.all_to_all(wide, ROW + COL, 0, 0, axis_index_groups=near_rows(), tile...  21.5 us
    pallas_call x14, Pallas kernels, call(): pl.pallas_call(body, name=name, out_shape=[jax.ShapeDtypeStruct(s, f32) f...  8.61 us

profile of v5, /device:TPU:2, one launch (start us, length us, event | category | flops | bytes accessed | tf_op | source)
XLA Modules:
  0.0 183.8 jit_solution(12385508045536308616)
XLA Ops:
  0.6 0.0 copy-start.6
  0.6 0.0 copy-start.7
  0.7 2.5 %first_products.1 = (f32[256,128]{1,0:T(8,128)S(1)}, f32[2,8,128]{2,1,0:T(8,128)S(1)}, f32[4,2,256,256]{3,2,1,0:T(8,128)S(1)}, f32[4,2,256,256]{3,2,1,0:T(8,128)S(1)}) custom-call(s32[1,2]{1,0:T(1,128)} %offsets.5, s32[2,4]{1,0:T(2,128)} %bitcast.88, f32[4,2,256,256]{3,2,1,0:T(8,128)} %A_in.1, f32[4,2,256,256]{3,2,1,0:T(8,128)} %G_in.1, f32[128,128]{1,0:T(8,128)} %bitcast.52), custom_call_target="tpu_custom_call" | custom-call | tf_op jit(solution)/shard_map/first_products/pallas_call | solution.py:26
  3.2 15.7 %all_to_all.65 = f32[16,1,2048]{2,1,0:T(1,128)S(1)} all-to-all(f32[16,1,2048]{2,1,0:T(1,128)S(1)} %bitcast.72), channel_id=1, replica_groups=mesh['row_0'=2,'row_1'=4,'row_2'=2,'col_0'=4,'col_1'=4] {'col_0','col_1'}, dimensions={0} | all-to-all | bytes 262144 | tf_op jit(solution)/shard_map/all_to_all | solution.py:352
  18.9 0.0 copy-done.6
  18.9 0.0 copy-done.7
  18.9 0.0 copy-start
  18.9 0.0 copy-start.1
  18.9 0.0 copy-start.2
  18.9 0.0 copy-start.3
  19.0 0.4 first_start.1
  19.4 18.9 %all_to_all.66 = f32[16,1,2048]{2,1,0:T(1,128)S(1)} all-to-all(f32[16,1,2048]{2,1,0:T(1,128)S(1)} %bitcast.73), channel_id=1, replica_groups=mesh['row_0'=2,'row_1'=4,'row_2'=2,'col_0'=4,'col_1'=4] {'row_0','row_1'..., dimensions={0} | all-to-all | bytes 262144 | tf_op jit(solution)/shard_map/all_to_all | solution.py:352
  38.2 0.0 copy-done
  38.2 0.0 copy-done.1
  38.2 0.0 copy-done.2
  38.2 0.0 copy-done.3
  38.3 0.5 begin_solve_0.1
  38.8 12.1 %all_to_all.67 = f32[16,1,2176]{2,1,0:T(1,128)S(1)} all-to-all(f32[16,1,2176]{2,1,0:T(1,128)S(1)} %bitcast.71), channel_id=1, replica_groups=mesh['row_0'=2,'row_1'=4,'row_2'=2,'col_0'=4,'col_1'=4] {'col_0','col_1'}, dimensions={0} | all-to-all | bytes 278528 | tf_op jit(solution)/shard_map/all_to_all | solution.py:352
  50.9 0.4 first_image.2
  51.3 13.3 %all_to_all.68 = f32[16,1,2176]{2,1,0:T(1,128)S(1)} all-to-all(f32[16,1,2176]{2,1,0:T(1,128)S(1)} %bitcast.66), channel_id=1, replica_groups=mesh['row_0'=2,'row_1'=4,'row_2'=2,'col_0'=4,'col_1'=4] {'row_0','row_1'..., dimensions={0} | all-to-all | bytes 278528 | tf_op jit(solution)/shard_map/all_to_all | solution.py:352
  64.6 0.0 copy-start.4
  64.6 0.0 copy-start.5
  64.6 0.6 first_step.2
  65.1 12.2 %all_to_all.69 = f32[16,1,2176]{2,1,0:T(1,128)S(1)} all-to-all(f32[16,1,2176]{2,1,0:T(1,128)S(1)} %bitcast.69), channel_id=1, replica_groups=mesh['row_0'=2,'row_1'=4,'row_2'=2,'col_0'=4,'col_1'=4] {'col_0','col_1'}, dimensions={0} | all-to-all | bytes 278528 | tf_op jit(solution)/shard_map/all_to_all | solution.py:352
  77.4 0.2 second_images.2
  77.6 10.7 %all_to_all.70 = f32[16,1,128]{2,1,0:T(1,128)S(1)} all-to-all(f32[16,1,128]{2,1,0:T(1,128)S(1)} %bitcast.86), channel_id=1, replica_groups={{0,16,32,48,64,80,96,112,130,146,162,178,194,210,226,242},{1,17,33,49,6..., dimensions={0} | all-to-all | bytes 16384 | tf_op jit(solution)/shard_map/all_to_all | solution.py:365
  88.3 0.0 copy-done.4
  88.3 0.0 copy-done.5
  88.3 0.8 update_0.1
  89.1 14.0 %all_to_all.71 = f32[16,1,3072]{2,1,0:T(1,128)S(1)} all-to-all(f32[16,1,3072]{2,1,0:T(1,128)S(1)} %bitcast.64), channel_id=1, replica_groups=mesh['row_0'=2,'row_1'=4,'row_2'=2,'col_0'=4,'col_1'=4] {'row_0','row_1'..., dimensions={0} | all-to-all | bytes 393216 | tf_op jit(solution)/shard_map/all_to_all | solution.py:352
  103.1 0.5 begin_solve_1.1
  103.7 14.5 %all_to_all.72 = f32[16,1,2176]{2,1,0:T(1,128)S(1)} all-to-all(f32[16,1,2176]{2,1,0:T(1,128)S(1)} %bitcast.67), channel_id=1, replica_groups=mesh['row_0'=2,'row_1'=4,'row_2'=2,'col_0'=4,'col_1'=4] {'col_0','col_1'}, dimensions={0} | all-to-all | bytes 278528 | tf_op jit(solution)/shard_map/all_to_all | solution.py:352
  118.1 0.4 first_image.3
  118.5 13.3 %all_to_all.73 = f32[16,1,2176]{2,1,0:T(1,128)S(1)} all-to-all(f32[16,1,2176]{2,1,0:T(1,128)S(1)} %bitcast.68), channel_id=1, replica_groups=mesh['row_0'=2,'row_1'=4,'row_2'=2,'col_0'=4,'col_1'=4] {'row_0','row_1'..., dimensions={0} | all-to-all | bytes 278528 | tf_op jit(solution)/shard_map/all_to_all | solution.py:352
  131.8 0.6 first_step.3
  132.4 12.2 %all_to_all.74 = f32[16,1,2176]{2,1,0:T(1,128)S(1)} all-to-all(f32[16,1,2176]{2,1,0:T(1,128)S(1)} %bitcast.70), channel_id=1, replica_groups=mesh['row_0'=2,'row_1'=4,'row_2'=2,'col_0'=4,'col_1'=4] {'col_0','col_1'}, dimensions={0} | all-to-all | bytes 278528 | tf_op jit(solution)/shard_map/all_to_all | solution.py:352
  144.6 0.2 second_images.3
  144.8 10.7 %all_to_all.75 = f32[16,1,128]{2,1,0:T(1,128)S(1)} all-to-all(f32[16,1,128]{2,1,0:T(1,128)S(1)} %bitcast.87), channel_id=1, replica_groups={{0,16,32,48,64,80,96,112,130,146,162,178,194,210,226,242},{1,17,33,49,6..., dimensions={0} | all-to-all | bytes 16384 | tf_op jit(solution)/shard_map/all_to_all | solution.py:365
  155.6 0.6 update_1.1
  156.2 13.5 %all_to_all.76 = f32[16,1,2176]{2,1,0:T(1,128)S(1)} all-to-all(f32[16,1,2176]{2,1,0:T(1,128)S(1)} %bitcast.65), channel_id=1, replica_groups=mesh['row_0'=2,'row_1'=4,'row_2'=2,'col_0'=4,'col_1'=4] {'row_0','row_1'..., dimensions={0} | all-to-all | bytes 278528 | tf_op jit(solution)/shard_map/all_to_all | solution.py:352
  169.7 0.2 last_dual.1
  169.9 13.3 %all_to_all.77 = f32[16,1,128]{2,1,0:T(1,128)S(1)} all-to-all(f32[16,1,128]{2,1,0:T(1,128)S(1)} %bitcast.76), channel_id=1, replica_groups=mesh['row_0'=2,'row_1'=4,'row_2'=2,'col_0'=4,'col_1'=4] {'col_0','col_1'}, dimensions={0} | all-to-all | bytes 16384 | tf_op jit(solution)/shard_map/all_to_all | solution.py:352
  183.2 0.6 finish.1
Async XLA Ops:
  0.6 18.3 %copy-start.6 = (f32[1024]{0:T(1024)S(1)}, f32[1024]{0:T(1024)}, u32[]{:S(2)}) copy-start(f32[1024]{0:T(1024)} %param.20) | copy-start | bytes 12292
  0.6 18.3 %copy-start.7 = (f32[1024]{0:T(1024)S(1)}, f32[1024]{0:T(1024)}, u32[]{:S(2)}) copy-start(f32[1024]{0:T(1024)} %param.21) | copy-start | bytes 12292
  18.9 19.3 %copy-start = (f32[16384]{0:T(1024)S(1)}, f32[16384]{0:T(1024)}, u32[]{:S(2)}) copy-start(f32[16384]{0:T(1024)} %param.16) | copy-start | bytes 196612
  18.9 19.3 %copy-start.1 = (f32[16384]{0:T(1024)S(1)}, f32[16384]{0:T(1024)}, u32[]{:S(2)}) copy-start(f32[16384]{0:T(1024)} %param.15) | copy-start | bytes 196612
  18.9 19.3 %copy-start.2 = (f32[16384]{0:T(1024)S(1)}, f32[16384]{0:T(1024)}, u32[]{:S(2)}) copy-start(f32[16384]{0:T(1024)} %param.19) | copy-start | bytes 196612
  18.9 19.3 %copy-start.3 = (s32[1,2]{1,0:T(1,128)S(1)}, s32[1,2]{1,0:T(1,128)}, u32[]{:S(2)}) copy-start(s32[1,2]{1,0:T(1,128)} %offsets.5) | copy-start | bytes 28
  64.6 23.8 %copy-start.4 = (f32[1024]{0:T(1024)S(1)}, f32[1024]{0:T(1024)}, u32[]{:S(2)}) copy-start(f32[1024]{0:T(1024)} %param.17) | copy-start | bytes 12292
  64.6 23.8 %copy-start.5 = (f32[1024]{0:T(1024)S(1)}, f32[1024]{0:T(1024)}, u32[]{:S(2)}) copy-start(f32[1024]{0:T(1024)} %param.18) | copy-start | bytes 12292

commit v6 on v5

--- a/solution.py
+++ b/solution.py
@@ -413,7 +413,7 @@
         out, gd2, ad2, small = kernel_call(second_images, "second_images", [payload(1), R8, R8, ONE])(
             recv, gd, ad, sc
         )
-        recv = exchange_near(out)
+        recv = exchange(out, ROW) if outer else exchange_near(out)
         args = (A, G, pat, recv, small, step, gd, ad, gd2, ad2, gx, ax, x, rem, d, z, y, lo, hi)
         if outer == 0:
 

time: 185 us -> 185 us (level)
    all_to_all x11 -> x12, blocking collectives: 153 us -> 164 us  [exchange(): return lax.all_to_all(wide, axes, 0, 0, tiled=True).reshape(a.shape)]
    all_to_all x2 -> x1, blocking collectives: 21.5 us -> 10.7 us  [exchange_near(): lax.all_to_all(wide, ROW + COL, 0, 0, axis_index_groups=near_rows(), tile...]
where the time goes in v6:
time: 185 us; the launch traced here: 184 us
  blocking collectives  174 us (94%)
  Pallas kernels  8.61 us (5%)
    all_to_all x12, blocking collectives, exchange(): return lax.all_to_all(wide, axes, 0, 0, tiled=True).reshape(a.shape)  164 us
    all_to_all x1, blocking collectives, exchange_near(): lax.all_to_all(wide, ROW + COL, 0, 0, axis_index_groups=near_rows(), tile...  10.7 us
    pallas_call x14, Pallas kernels, call(): pl.pallas_call(body, name=name, out_shape=[jax.ShapeDtypeStruct(s, f32) f...  8.61 us

profile of v6, /device:TPU:2, one launch (start us, length us, event | category | flops | bytes accessed | tf_op | source)
XLA Modules:
  0.0 183.8 jit_solution(4641478700104125900)
XLA Ops:
  0.6 0.0 copy-start.6
  0.6 0.0 copy-start.7
  0.7 2.5 %first_products.1 = (f32[256,128]{1,0:T(8,128)S(1)}, f32[2,8,128]{2,1,0:T(8,128)S(1)}, f32[4,2,256,256]{3,2,1,0:T(8,128)S(1)}, f32[4,2,256,256]{3,2,1,0:T(8,128)S(1)}) custom-call(s32[1,2]{1,0:T(1,128)} %offsets.5, s32[2,4]{1,0:T(2,128)} %bitcast.88, f32[4,2,256,256]{3,2,1,0:T(8,128)} %A_in.1, f32[4,2,256,256]{3,2,1,0:T(8,128)} %G_in.1, f32[128,128]{1,0:T(8,128)} %bitcast.52), custom_call_target="tpu_custom_call" | custom-call | tf_op jit(solution)/shard_map/first_products/pallas_call | solution.py:26
  3.2 15.7 %all_to_all.65 = f32[16,1,2048]{2,1,0:T(1,128)S(1)} all-to-all(f32[16,1,2048]{2,1,0:T(1,128)S(1)} %bitcast.72), channel_id=1, replica_groups=mesh['row_0'=2,'row_1'=4,'row_2'=2,'col_0'=4,'col_1'=4] {'col_0','col_1'}, dimensions={0} | all-to-all | bytes 262144 | tf_op jit(solution)/shard_map/all_to_all | solution.py:352
  18.9 0.0 copy-done.6
  18.9 0.0 copy-done.7
  18.9 0.0 copy-start
  18.9 0.0 copy-start.1
  18.9 0.0 copy-start.2
  18.9 0.0 copy-start.3
  19.0 0.4 first_start.1
  19.4 18.9 %all_to_all.66 = f32[16,1,2048]{2,1,0:T(1,128)S(1)} all-to-all(f32[16,1,2048]{2,1,0:T(1,128)S(1)} %bitcast.73), channel_id=1, replica_groups=mesh['row_0'=2,'row_1'=4,'row_2'=2,'col_0'=4,'col_1'=4] {'row_0','row_1'..., dimensions={0} | all-to-all | bytes 262144 | tf_op jit(solution)/shard_map/all_to_all | solution.py:352
  38.2 0.0 copy-done
  38.2 0.0 copy-done.1
  38.2 0.0 copy-done.2
  38.2 0.0 copy-done.3
  38.3 0.5 begin_solve_0.1
  38.8 12.1 %all_to_all.67 = f32[16,1,2176]{2,1,0:T(1,128)S(1)} all-to-all(f32[16,1,2176]{2,1,0:T(1,128)S(1)} %bitcast.71), channel_id=1, replica_groups=mesh['row_0'=2,'row_1'=4,'row_2'=2,'col_0'=4,'col_1'=4] {'col_0','col_1'}, dimensions={0} | all-to-all | bytes 278528 | tf_op jit(solution)/shard_map/all_to_all | solution.py:352
  50.9 0.4 first_image.2
  51.3 13.3 %all_to_all.68 = f32[16,1,2176]{2,1,0:T(1,128)S(1)} all-to-all(f32[16,1,2176]{2,1,0:T(1,128)S(1)} %bitcast.66), channel_id=1, replica_groups=mesh['row_0'=2,'row_1'=4,'row_2'=2,'col_0'=4,'col_1'=4] {'row_0','row_1'..., dimensions={0} | all-to-all | bytes 278528 | tf_op jit(solution)/shard_map/all_to_all | solution.py:352
  64.6 0.0 copy-start.4
  64.6 0.0 copy-start.5
  64.6 0.6 first_step.2
  65.1 12.2 %all_to_all.69 = f32[16,1,2176]{2,1,0:T(1,128)S(1)} all-to-all(f32[16,1,2176]{2,1,0:T(1,128)S(1)} %bitcast.69), channel_id=1, replica_groups=mesh['row_0'=2,'row_1'=4,'row_2'=2,'col_0'=4,'col_1'=4] {'col_0','col_1'}, dimensions={0} | all-to-all | bytes 278528 | tf_op jit(solution)/shard_map/all_to_all | solution.py:352
  77.4 0.2 second_images.2
  77.6 10.7 %all_to_all.70 = f32[16,1,128]{2,1,0:T(1,128)S(1)} all-to-all(f32[16,1,128]{2,1,0:T(1,128)S(1)} %bitcast.86), channel_id=1, replica_groups={{0,16,32,48,64,80,96,112,130,146,162,178,194,210,226,242},{1,17,33,49,6..., dimensions={0} | all-to-all | bytes 16384 | tf_op jit(solution)/shard_map/all_to_all | solution.py:365
  88.3 0.0 copy-done.4
  88.3 0.0 copy-done.5
  88.3 0.8 update_0.1
  89.1 14.0 %all_to_all.71 = f32[16,1,3072]{2,1,0:T(1,128)S(1)} all-to-all(f32[16,1,3072]{2,1,0:T(1,128)S(1)} %bitcast.64), channel_id=1, replica_groups=mesh['row_0'=2,'row_1'=4,'row_2'=2,'col_0'=4,'col_1'=4] {'row_0','row_1'..., dimensions={0} | all-to-all | bytes 393216 | tf_op jit(solution)/shard_map/all_to_all | solution.py:352
  103.1 0.5 begin_solve_1.1
  103.7 14.5 %all_to_all.72 = f32[16,1,2176]{2,1,0:T(1,128)S(1)} all-to-all(f32[16,1,2176]{2,1,0:T(1,128)S(1)} %bitcast.67), channel_id=1, replica_groups=mesh['row_0'=2,'row_1'=4,'row_2'=2,'col_0'=4,'col_1'=4] {'col_0','col_1'}, dimensions={0} | all-to-all | bytes 278528 | tf_op jit(solution)/shard_map/all_to_all | solution.py:352
  118.1 0.4 first_image.3
  118.5 13.3 %all_to_all.73 = f32[16,1,2176]{2,1,0:T(1,128)S(1)} all-to-all(f32[16,1,2176]{2,1,0:T(1,128)S(1)} %bitcast.68), channel_id=1, replica_groups=mesh['row_0'=2,'row_1'=4,'row_2'=2,'col_0'=4,'col_1'=4] {'row_0','row_1'..., dimensions={0} | all-to-all | bytes 278528 | tf_op jit(solution)/shard_map/all_to_all | solution.py:352
  131.8 0.6 first_step.3
  132.4 12.2 %all_to_all.74 = f32[16,1,2176]{2,1,0:T(1,128)S(1)} all-to-all(f32[16,1,2176]{2,1,0:T(1,128)S(1)} %bitcast.70), channel_id=1, replica_groups=mesh['row_0'=2,'row_1'=4,'row_2'=2,'col_0'=4,'col_1'=4] {'col_0','col_1'}, dimensions={0} | all-to-all | bytes 278528 | tf_op jit(solution)/shard_map/all_to_all | solution.py:352
  144.6 0.2 second_images.3
  144.8 12.5 %all_to_all.75 = f32[16,1,128]{2,1,0:T(1,128)S(1)} all-to-all(f32[16,1,128]{2,1,0:T(1,128)S(1)} %bitcast.87), channel_id=1, replica_groups=mesh['row_0'=2,'row_1'=4,'row_2'=2,'col_0'=4,'col_1'=4] {'row_0','row_1'..., dimensions={0} | all-to-all | bytes 16384 | tf_op jit(solution)/shard_map/all_to_all | solution.py:352
  157.4 0.6 update_1.1
  158.0 13.3 %all_to_all.76 = f32[16,1,2176]{2,1,0:T(1,128)S(1)} all-to-all(f32[16,1,2176]{2,1,0:T(1,128)S(1)} %bitcast.65), channel_id=1, replica_groups=mesh['row_0'=2,'row_1'=4,'row_2'=2,'col_0'=4,'col_1'=4] {'row_0','row_1'..., dimensions={0} | all-to-all | bytes 278528 | tf_op jit(solution)/shard_map/all_to_all | solution.py:352
  171.3 0.2 last_dual.1
  171.5 11.7 %all_to_all.77 = f32[16,1,128]{2,1,0:T(1,128)S(1)} all-to-all(f32[16,1,128]{2,1,0:T(1,128)S(1)} %bitcast.76), channel_id=1, replica_groups=mesh['row_0'=2,'row_1'=4,'row_2'=2,'col_0'=4,'col_1'=4] {'col_0','col_1'}, dimensions={0} | all-to-all | bytes 16384 | tf_op jit(solution)/shard_map/all_to_all | solution.py:352
  183.2 0.6 finish.1
Async XLA Ops:
  0.6 18.3 %copy-start.6 = (f32[1024]{0:T(1024)S(1)}, f32[1024]{0:T(1024)}, u32[]{:S(2)}) copy-start(f32[1024]{0:T(1024)} %param.20) | copy-start | bytes 12292
  0.6 18.3 %copy-start.7 = (f32[1024]{0:T(1024)S(1)}, f32[1024]{0:T(1024)}, u32[]{:S(2)}) copy-start(f32[1024]{0:T(1024)} %param.21) | copy-start | bytes 12292
  18.9 19.3 %copy-start = (f32[16384]{0:T(1024)S(1)}, f32[16384]{0:T(1024)}, u32[]{:S(2)}) copy-start(f32[16384]{0:T(1024)} %param.16) | copy-start | bytes 196612
  18.9 19.3 %copy-start.1 = (f32[16384]{0:T(1024)S(1)}, f32[16384]{0:T(1024)}, u32[]{:S(2)}) copy-start(f32[16384]{0:T(1024)} %param.15) | copy-start | bytes 196612
  18.9 19.3 %copy-start.2 = (f32[16384]{0:T(1024)S(1)}, f32[16384]{0:T(1024)}, u32[]{:S(2)}) copy-start(f32[16384]{0:T(1024)} %param.19) | copy-start | bytes 196612
  18.9 19.3 %copy-start.3 = (s32[1,2]{1,0:T(1,128)S(1)}, s32[1,2]{1,0:T(1,128)}, u32[]{:S(2)}) copy-start(s32[1,2]{1,0:T(1,128)} %offsets.5) | copy-start | bytes 28
  64.6 23.8 %copy-start.4 = (f32[1024]{0:T(1024)S(1)}, f32[1024]{0:T(1024)}, u32[]{:S(2)}) copy-start(f32[1024]{0:T(1024)} %param.17) | copy-start | bytes 12292
  64.6 23.8 %copy-start.5 = (f32[1024]{0:T(1024)S(1)}, f32[1024]{0:T(1024)}, u32[]{:S(2)}) copy-start(f32[1024]{0:T(1024)} %param.18) | copy-start | bytes 12292
